TPU v7x, 8 devices: a whole 2x2x1 slice. The times are simulated.
8 devices in a mesh: dp: 2 (over z, y), cp: 4 (over x, core).
Axes of the slice: x: 2, y: 2, z: 1, core: 2. Of those that a mesh axis runs over, the one named last changes fastest.
Arguments:
- hidden: bfloat16 [8192, 4096], P(('dp', 'cp')), parts along dimension 0
- seg_id: int32 [8192], P(('dp', 'cp')), parts along dimension 0
- doc_pos: int32 [8192], P(('dp', 'cp')), parts along dimension 0
- norm_gain: bfloat16 [4096], replicated
- w_qkv: bfloat16 [4096, 4608], replicated
- b_qkv: bfloat16 [4608], replicated
- w_out: bfloat16 [4096, 4096], replicated
- grad_out: bfloat16 [8192, 4096], P(('dp', 'cp')), parts along dimension 0
Outputs:
- output 1: bfloat16 [8192, 4096], P(('dp', 'cp')), parts along dimension 0
- output 2: bfloat16 [8192, 4096], P(('dp', 'cp')), parts along dimension 0
- output 3: float32 [8192], P('dp'), parts along dimension 0
- output 4: float32 [8192, 4608], P('dp'), parts along dimension 0
- output 5: float32 [9216], P('dp'), parts along dimension 0
- output 6: float32 [8192, 4096], P('dp'), parts along dimension 0
There are 2 independent parts. A program takes and returns all parts, laid end to end along the dimension named above; an argument that names none is the same for every part.
All inputs are finite; a program needn't handle non-finite values.
Results may differ from a plain program's by a relative error of at most 0.0186529.
Values are sent between devices in bfloat16 or wider.
A program may use at most 1 GiB of HBM per device.

v0:
```python
import jax
import jax.numpy as jnp
from jax import lax
from jax.sharding import PartitionSpec as P

HEAD_DIM = 128
ROT_DIMS = 64
ROPE_BASE = 5000000.0
EPS_NORM = 1e-5
NEG_BIG = -1e30


def rotate(values, cos_ang, sin_ang):
    rot_pairs = values[..., :ROT_DIMS].reshape(values.shape[:-1] + (ROT_DIMS // 2, 2))
    even_part = rot_pairs[..., 0]
    odd_part = rot_pairs[..., 1]
    turned = jnp.stack([even_part * cos_ang - odd_part * sin_ang, odd_part * cos_ang + even_part * sin_ang], axis=-1)
    return jnp.concatenate([turned.reshape(values.shape[:-1] + (ROT_DIMS,)), values[..., ROT_DIMS:]], axis=-1)


def block_mask(seg_q, seg_k, q_start, k_start):
    q_index = q_start + jnp.arange(seg_q.shape[0])[:, None]
    k_index = k_start + jnp.arange(seg_k.shape[0])[None, :]
    return (seg_q[:, None] == seg_k[None, :]) & (k_index <= q_index)


def forward_update(run_state, q_rot, k_blk, v_blk, vis_mask):
    m_run, l_run, acc_sum = run_state
    scores = jnp.einsum('qgrd,kgd->grqk', q_rot, k_blk, preferred_element_type=jnp.float32) * (HEAD_DIM ** -0.5)
    scores = jnp.where(vis_mask, scores, NEG_BIG)
    m_new = jnp.maximum(m_run, jnp.max(scores, axis=-1))
    p_mat = jnp.where(vis_mask, jnp.exp(scores - m_new[..., None]), 0.0)
    rescale = jnp.exp(m_run - m_new)
    l_new = l_run * rescale + jnp.sum(p_mat, axis=-1)
    acc_new = acc_sum * rescale[..., None] + jnp.einsum('grqk,kgd->grqd', p_mat.astype(jnp.bfloat16), v_blk, preferred_element_type=jnp.float32)
    return m_new, l_new, acc_new


def backward_update(q_rot, k_blk, v_blk, vis_mask, log_norm, grad_ctx, row_dot):
    scale = HEAD_DIM ** -0.5
    scores = jnp.einsum('qgrd,kgd->grqk', q_rot, k_blk, preferred_element_type=jnp.float32) * scale
    p_mat = jnp.where(vis_mask, jnp.exp(jnp.where(vis_mask, scores, NEG_BIG) - log_norm[..., None]), 0.0)
    d_value = jnp.einsum('grqk,grqd->kgd', p_mat.astype(jnp.bfloat16), grad_ctx, preferred_element_type=jnp.float32)
    d_prob = jnp.einsum('grqd,kgd->grqk', grad_ctx, v_blk, preferred_element_type=jnp.float32)
    d_score = (p_mat * (d_prob - row_dot[..., None])).astype(jnp.bfloat16)
    d_query = jnp.einsum('grqk,kgd->qgrd', d_score, k_blk, preferred_element_type=jnp.float32) * scale
    d_key = jnp.einsum('grqk,qgrd->kgd', d_score, q_rot, preferred_element_type=jnp.float32) * scale
    return d_query, d_key, d_value


def solution(mesh):
    n_ctx = mesh.shape['cp']
    shift_perm = [(src_dev, (src_dev + 1) % n_ctx) for src_dev in range(n_ctx)]

    def per_device(hidden, seg_id, doc_pos, norm_gain, w_qkv, b_qkv, w_out, grad_out):
        n_rows, hid_width = hidden.shape
        att_width = w_out.shape[0]
        kv_width = (w_qkv.shape[1] - att_width) // 2
        groups = kv_width // HEAD_DIM
        n_rep = att_width // kv_width
        my_index = lax.axis_index('cp')
        q_start = my_index * n_rows
        hid_f32 = hidden.astype(jnp.float32)
        inv_rms = lax.rsqrt(jnp.mean(hid_f32 * hid_f32, axis=-1, keepdims=True) + EPS_NORM)
        x_hat = hid_f32 * inv_rms
        gain_f32 = norm_gain.astype(jnp.float32)
        normed = (x_hat * gain_f32).astype(jnp.bfloat16)
        qkv_out = (jnp.dot(normed, w_qkv, preferred_element_type=jnp.float32) + b_qkv.astype(jnp.float32)).astype(jnp.bfloat16)
        inv_freq = ROPE_BASE ** (-jnp.arange(0, ROT_DIMS, 2).astype(jnp.float32) / ROT_DIMS)
        angles = doc_pos.astype(jnp.float32)[:, None] * inv_freq[None, :]
        cos_q = jnp.cos(angles)[:, None, None, :]
        sin_q = jnp.sin(angles)[:, None, None, :]
        cos_k = jnp.cos(angles)[:, None, :]
        sin_k = jnp.sin(angles)[:, None, :]
        q_rot = rotate(qkv_out[:, :att_width].astype(jnp.float32).reshape(n_rows, groups, n_rep, HEAD_DIM), cos_q, sin_q).astype(jnp.bfloat16)
        k_rot = rotate(qkv_out[:, att_width:att_width + kv_width].astype(jnp.float32).reshape(n_rows, groups, HEAD_DIM), cos_k, sin_k).astype(jnp.bfloat16)
        v_val = qkv_out[:, att_width + kv_width:].reshape(n_rows, groups, HEAD_DIM)

        def fwd_visit(run_state, k_blk, v_blk, seg_k, src_idx, is_live):
            vis_mask = block_mask(seg_id, seg_k, q_start, src_idx * n_rows)
            return lax.cond(is_live & jnp.any(vis_mask),
                            lambda st_in: forward_update(st_in, q_rot, k_blk, v_blk, vis_mask),
                            lambda st_in: st_in, run_state)

        init_state = (
            jnp.full((groups, n_rep, n_rows), NEG_BIG, jnp.float32),
            jnp.zeros((groups, n_rep, n_rows), jnp.float32),
            jnp.zeros((groups, n_rep, n_rows, HEAD_DIM), jnp.float32),
        )
        run_state = fwd_visit(init_state, k_rot, v_val, seg_id, my_index, True)

        def fwd_turn(turn_idx, loop_vals):
            run_state, k_blk, v_blk, seg_k = loop_vals
            k_blk, v_blk, seg_k = lax.ppermute((k_blk, v_blk, seg_k), 'cp', shift_perm)
            run_state = fwd_visit(run_state, k_blk, v_blk, seg_k, my_index - turn_idx, turn_idx <= my_index)
            return run_state, k_blk, v_blk, seg_k

        run_state = lax.fori_loop(1, n_ctx, fwd_turn, (run_state, k_rot, v_val, seg_id))[0]
        m_run, l_run, acc_sum = run_state
        context = (acc_sum / l_run[..., None]).astype(jnp.bfloat16)
        log_norm = m_run + jnp.log(l_run)
        w_out4 = w_out.reshape(groups, n_rep, HEAD_DIM, hid_width)
        y_out = (hid_f32 + jnp.einsum('grqd,grdn->qn', context, w_out4, preferred_element_type=jnp.float32)).astype(jnp.bfloat16)

        grad_ctx = jnp.einsum('qn,grdn->grqd', grad_out, w_out4, preferred_element_type=jnp.float32).astype(jnp.bfloat16)
        grad_wout = jnp.einsum('grqd,qn->grdn', context, grad_out, preferred_element_type=jnp.float32).reshape(att_width, hid_width)
        row_dot = jnp.einsum('grqd,grqd->grq', grad_ctx, context, preferred_element_type=jnp.float32)

        def bwd_visit(grad_acc, k_blk, v_blk, seg_k, src_idx, is_live):
            vis_mask = block_mask(seg_id, seg_k, q_start, src_idx * n_rows)

            def absorb(acc_in):
                d_query, d_key, d_value = backward_update(q_rot, k_blk, v_blk, vis_mask, log_norm, grad_ctx, row_dot)
                return acc_in[0] + d_query, acc_in[1] + d_key, acc_in[2] + d_value

            return lax.cond(is_live & jnp.any(vis_mask), absorb, lambda acc_in: acc_in, grad_acc)

        zero_kv = jnp.zeros((n_rows, groups, HEAD_DIM), jnp.float32)
        grad_acc = bwd_visit((jnp.zeros((n_rows, groups, n_rep, HEAD_DIM), jnp.float32), zero_kv, zero_kv),
                             k_rot, v_val, seg_id, my_index, True)

        def bwd_turn(turn_idx, loop_vals):
            d_query, d_key, d_value, k_blk, v_blk, seg_k = loop_vals
            k_blk, v_blk, seg_k, d_key, d_value = lax.ppermute((k_blk, v_blk, seg_k, d_key, d_value), 'cp', shift_perm)
            d_query, d_key, d_value = bwd_visit((d_query, d_key, d_value), k_blk, v_blk, seg_k, my_index - turn_idx, turn_idx <= my_index)
            return d_query, d_key, d_value, k_blk, v_blk, seg_k

        d_query, d_key, d_value, _, _, _ = lax.fori_loop(1, n_ctx, bwd_turn, grad_acc + (k_rot, v_val, seg_id))
        d_key, d_value = lax.ppermute((d_key, d_value), 'cp', shift_perm)

        grad_qkv = jnp.concatenate([
            rotate(d_query, cos_q, -sin_q).reshape(n_rows, att_width),
            rotate(d_key, cos_k, -sin_k).reshape(n_rows, kv_width),
            d_value.reshape(n_rows, kv_width)], axis=1).astype(jnp.bfloat16)
        grad_bqkv = jnp.sum(grad_qkv.astype(jnp.float32), axis=0)
        grad_wqkv = jnp.einsum('qn,qc->nc', normed, grad_qkv, preferred_element_type=jnp.float32)
        grad_normed = jnp.einsum('qc,nc->qn', grad_qkv, w_qkv, preferred_element_type=jnp.float32)
        grad_gain = jnp.sum(grad_normed * x_hat, axis=0)
        scaled = grad_normed * gain_f32
        grad_hidden = (grad_out.astype(jnp.float32) + inv_rms * (scaled - x_hat * jnp.mean(scaled * x_hat, axis=-1, keepdims=True))).astype(jnp.bfloat16)
        grad_gain, grad_wqkv, grad_bqkv, grad_wout = lax.psum((grad_gain, grad_wqkv, grad_bqkv, grad_wout), 'cp')
        return y_out, grad_hidden, grad_gain, grad_wqkv, grad_bqkv, grad_wout

    act_spec = P(('dp', 'cp'), None)
    row_spec = P(('dp', 'cp'))
    return jax.shard_map(per_device, mesh=mesh,
                         in_specs=(act_spec, row_spec, row_spec, P(), P(), P(), P(), act_spec),
                         out_specs=(act_spec, act_spec, P('dp'), P('dp', None), P('dp'), P('dp', None)),
                         check_vma=False)
```

profile of v0, /device:TPU:0, one launch (start us, length us, event | category | flops | bytes accessed | tf_op | source)
XLA Modules:
  0.0 3384.8 jit_solution(3437043746498805297)
XLA Ops:
  13.7 45.6 %add_convert_fusion = bf16[1024,4608]{1,0:T(8,128)(2,1)S(1)} fusion(bf16[4096,4608]{1,0:T(8,128)(2,1)} %param.24, f32[4608]{0:T(1024)S(1)} %convert_element_type.91, bf16[1024,4096]{1,0:T(8,128)(2,1)} %param.20, f32[4096]{0:T(1024)S(1)} %convert_element_type.89, f32[1024]{0:T(1024)S(1)} %add_rsqrt_fusion), kind=kOutput, calls=%fused_computation.87 | convolution fusion | flops 38680920064 | bytes 55613440 | tf_op jit(solution)/shard_map/dot_general | solution.py:68
  160.7 42.9 %convert_bitcast_fusion = bf16[2,16,1024,128]{2,3,1,0:T(8,128)(2,1)} fusion(bf16[2,16,128,4096]{3,2,1,0:T(8,128)(2,1)} %bitcast.212, bf16[1024,4096]{1,0:T(8,128)(2,1)} %param.27), kind=kOutput, calls=%fused_computation.108 | convolution fusion | flops 34363932672 | bytes 50331648 | tf_op jit(solution)/shard_map/qn,grdn->grqd/dot_general | solution.py:105
  216.7 173.5 %conditional.4 = (f32[2,16,1024]{2,1,0:T(8,128)}, f32[2,16,1024]{2,1,0:T(8,128)S(1)}, f32[2,16,1024,128]{3,2,1,0:T(8,128)}) conditional(s32[]{:T(128)} %convert_element_type.88, () %tuple.66, (pred[1024,1024]{0,1:T(8,128)(4,1)S(1)}, bf16[1024,2,128]{0,1,2:T(2,128)(2,1)S(1)}, bf16[1024,2,16,128]{0,2,3,1:T(8,128)(2,1)}, ...), branch_computations={%region_2.0_spmd, %region_3.6_spmd} | conditional | flops 17620402176 | bytes 433455136 | solution.py:81
  216.7 74.5 %fusion = (f32[2,16,1024]{2,1,0:T(8,128)S(1)}, f32[2,1024,1024,16]{2,1,3,0:T(8,128)}) fusion(pred[1024,1024]{0,1:T(8,128)(4,1)S(1)} %get-tuple-element.464, bf16[1024,2,16,128]{0,2,3,1:T(8,128)(2,1)} %get-tuple-element.593, bf16[1024,2,128,1]{0,1,2,3:T(2,128)(2,1)S(1)} %bitcast.199), kind=kOutput, calls=%fused_computation.2 | convolution fusion | flops 8690565120 | bytes 144310272 | tf_op jit(solution)/shard_map/cond/branch_1_fun/qgrd,kgd->grqk/dot_general | solution.py:29
  333.3 55.6 %broadcast_add_fusion = f32[2,16,1024,128]{3,2,1,0:T(8,128)} fusion(f32[2,16,1024]{2,1,0:T(8,128)S(1)} %get-tuple-element.681, f32[2,1024,1024,16]{2,1,3,0:T(8,128)} %get-tuple-element.692, f32[2,16,1024]{2,1,0:T(8,128)} %get-tuple-element.903, pred[1024,1024]{0,1:T(8,128)(4,1)S(1)} %get-tuple-element.464, bf16[1024,2,128,1]{2,1,0,3:T(2,128)(2,1)S(1)} %bitcast.210), kind=kOutput, calls=%fused_computation.9 | convolution fusion | flops 8761901056 | bytes 152829952 | tf_op jit(solution)/shard_map/cond/branch_1_fun/grqk,kgd->grqd/dot_general | solution.py:35
  390.9 342.7 %while.46 = (s32[]{:T(128)}, f32[2,16,1024]{2,1,0:T(8,128)}, f32[2,16,1024]{2,1,0:T(8,128)}, f32[2,16,1024,128]{3,2,1,0:T(8,128)}, bf16[1024,2,128]{2,0,1:T(8,12...) while((s32[]{:T(128)}, f32[2,16,1024]{2,1,0:T(8,128)}, ...), condition=%wide.region_12.13_spmd, body=%wide.region_6.12_spmd.sunk | while | flops 17628727296 | bytes 459342304 | solution.py:98
  407.0 149.4 %collective-permute-start = (s32[1024]{0:T(1024)S(1)}, s32[1024]{0:T(1024)S(1)}, u32[]{:S(2)}, u32[]{:S(2)}) collective-permute-start(s32[1024]{0:T(1024)S(1)} %get-tuple-element.925), channel_id=1, source_target_pairs={{0,1},{1,2},{2,3},{3,0},{4,5},{5,6},{6,7},{7,4}} | collective-permute-start | bytes 12296 | tf_op jit(solution)/shard_map/while/body/eval_jaxpr/ppermute | solution.py:94
  574.1 146.6 %collective-permute-start.1 = (bf16[1024,2,128]{2,0,1:T(8,128)(2,1)S(1)}, bf16[1024,2,128]{2,0,1:T(8,128)(2,1)S(1)}, u32[]{:S(2)}, u32[]{:S(2)}) collective-permute-start(bf16[1024,2,128]{2,0,1:T(8,128)(2,1)S(1)} %get-tuple-element.923), channel_id=1, source_target_pairs={{0,1},{1,2},{2,3},{3,0},{4,5},{5,6},{6,7},{7,4}} | collective-permute-start | bytes 1572872 | tf_op jit(solution)/shard_map/while/body/eval_jaxpr/ppermute | solution.py:94
  750.9 46.0 %fusion.82 = f32[2,16,128,4096]{3,2,1,0:T(8,128)} fusion(bf16[2,16,1024,128]{3,2,1,0:T(8,128)(2,1)} %get-tuple-element.690, bf16[1024,4096]{1,0:T(8,128)(2,1)} %param.27), kind=kOutput, calls=%fused_computation.104 | convolution fusion | flops 34359738368 | bytes 83886080 | tf_op jit(solution)/shard_map/grqd,qn->grdn/dot_general | solution.py:106
  811.8 255.2 %conditional.5 = (f32[1024,2,16,128]{3,0,2,1:T(8,128)}, f32[1024,2,128]{2,0,1:T(8,128)}, f32[1024,2,128]{2,0,1:T(8,128)}) conditional(s32[]{:T(128)} %convert_element_type.88, () %tuple.69, (pred[1024,1024]{0,1:T(8,128)(4,1)S(1)}, bf16[1024,2,128]{0,1,2:T(2,128)(2,1)S(1)}, bf16[1024,2,16,128]{0,2,3,1:T(8,128)(2,1)}, f32[2,16,1024]{2,1,0:T(8,128)}, ...), branch_computations={%region_13.14_spmd, %region_14.15_spmd} | conditional | flops 43356782592 | bytes 682491968 | solution.py:116
  824.9 47.9 %fusion.98 = f32[2,1024,1024,16]{2,1,3,0:T(8,128)} fusion(bf16[1024,2,128,1]{2,0,3,1:T(8,128)(2,1)S(1)} %copy.70, bf16[1024,2,16,128]{3,0,2,1:T(8,128)(2,1)} %copy.50), kind=kOutput, calls=%fused_computation.142 | convolution fusion | flops 8589934592 | bytes 143130624 | tf_op jit(solution)/shard_map/cond/branch_1_fun/qgrd,kgd->grqk/dot_general | solution.py:41
  872.8 47.1 %fusion.37 = f32[1024,2,128]{2,0,1:T(8,128)} fusion(bf16[2,16,1024,128]{2,3,1,0:T(8,128)(2,1)} %get-tuple-element.610, f32[2,1024,1024,16]{2,1,3,0:T(8,128)} %fusion.98, f32[2,16,1024]{2,1,0:T(8,128)} %get-tuple-element.493, pred[1024,1024]{0,1:T(8,128)(4,1)S(1)} %get-tuple-element.490), kind=kOutput, calls=%fused_computation.46 | convolution fusion | flops 8757706752 | bytes 144834560 | tf_op jit(solution)/shard_map/cond/branch_1_fun/grqk,grqd->kgd/dot_general | solution.py:43
  919.9 79.0 %multiply_convert_fusion = bf16[2,16,1024,1024]{2,3,1,0:T(8,128)(2,1)} fusion(f32[2,1024,1024,16]{2,1,3,0:T(8,128)} %fusion.98, f32[2,16,1024]{2,1,0:T(8,128)} %get-tuple-element.496, f32[2,16,1024]{2,1,0:T(8,128)} %get-tuple-element.493, pred[1024,1024]{0,1:T(8,128)(4,1)S(1)} %get-tuple-element.490, bf16[2,16,1024,128]{2,3,1,0:T(8,128)(2,1)} %get-tuple-element.610, ...), kind=kOutput, calls=%fused_computation.41 | convolution fusion | flops 8824815616 | bytes 211550208 | tf_op jit(solution)/shard_map/cond/branch_1_fun/grqd,kgd->grqk/dot_general | solution.py:44
  1067.1 813.6 %while.47 = (s32[]{:T(128)}, f32[1024,2,16,128]{3,0,2,1:T(8,128)}, f32[1024,2,128]{2,0,1:T(8,128)}, f32[1024,2,128]{2,0,1:T(8,128)}, bf16[1024,2,128]{2,0,1:T(8,...) while((s32[]{:T(128)}, f32[1024,2,16,128]{3,0,2,1:T(8,128)}, ...), condition=%wide.region_19.0_spmd, body=%wide.region_15.19_spmd.sunk | while | flops 43365699584 | bytes 728695424 | solution.py:128
  1069.4 68.2 %collective-permute-done.3 = s32[1024]{0:T(1024)S(1)} collective-permute-done((s32[1024]{0:T(1024)S(1)}, s32[1024]{0:T(1024)S(1)}, u32[]{:S(2)}, u32[]{:S(2)}) %collective-permute-start.3) | collective-permute-done | bytes 4128 | tf_op jit(solution)/shard_map/while/body/eval_jaxpr/ppermute | solution.py:124
  1176.4 248.5 %collective-permute-start.5 = (f32[1024,2,128]{2,0,1:T(8,128)}, f32[1024,2,128]{2,0,1:T(8,128)S(1)}, u32[]{:S(2)}, u32[]{:S(2)}) collective-permute-start(f32[1024,2,128]{2,0,1:T(8,128)} %get-tuple-element.970), channel_id=1, source_target_pairs={{0,1},{1,2},{2,3},{3,0},{4,5},{5,6},{6,7},{7,4}} | collective-permute-start | bytes 3145736 | tf_op jit(solution)/shard_map/while/body/eval_jaxpr/ppermute | solution.py:124
  1427.5 58.3 %collective-permute-done.3 = s32[1024]{0:T(1024)S(1)} collective-permute-done((s32[1024]{0:T(1024)S(1)}, s32[1024]{0:T(1024)S(1)}, u32[]{:S(2)}, u32[]{:S(2)}) %collective-permute-start.3) | collective-permute-done | bytes 4128 | tf_op jit(solution)/shard_map/while/body/eval_jaxpr/ppermute | solution.py:124
  1536.8 236.5 %collective-permute-start.3 = (s32[1024]{0:T(1024)S(1)}, s32[1024]{0:T(1024)S(1)}, u32[]{:S(2)}, u32[]{:S(2)}) collective-permute-start(s32[1024]{0:T(1024)S(1)} %get-tuple-element.973), channel_id=1, source_target_pairs={{0,1},{1,2},{2,3},{3,0},{4,5},{5,6},{6,7},{7,4}} | collective-permute-start | bytes 12296 | tf_op jit(solution)/shard_map/while/body/eval_jaxpr/ppermute | solution.py:124
  1773.3 68.2 %collective-permute-done.3 = s32[1024]{0:T(1024)S(1)} collective-permute-done((s32[1024]{0:T(1024)S(1)}, s32[1024]{0:T(1024)S(1)}, u32[]{:S(2)}, u32[]{:S(2)}) %collective-permute-start.3) | collective-permute-done | bytes 4128 | tf_op jit(solution)/shard_map/while/body/eval_jaxpr/ppermute | solution.py:124
  1939.5 58.9 %fusion.88 = f32[4096,4608]{1,0:T(8,128)} fusion(bf16[1024,4096]{1,0:T(8,128)(2,1)} %param.20, f32[4096]{0:T(1024)S(1)} %copy-done.29, f32[1024]{0:T(1024)S(1)} %copy-done.31, bf16[1024,256]{0,1:T(8,128)(2,1)S(1)} %bitcast.201, bf16[1024,256]{0,1:T(8,128)(2,1)S(1)} %bitcast.196, bf16[1024,4096]{0,1:T(8,128)(2,1)} %bitcast.187), kind=kOutput, calls=%fused_computation.116 | convolution fusion | flops 38699794432 | bytes 93343744 | tf_op jit(solution)/shard_map/qn,qc->nc/dot_general | solution.py:136
  2061.4 49.1 %fusion.79 = (f32[4096]{0:T(1024)S(1)}, f32[1024]{0:T(1024)S(1)}, f32[1024,4096]{1,0:T(8,128)}) fusion(bf16[1024,4096]{1,0:T(8,128)(2,1)S(1)} %bitcast.192, f32[1024]{0:T(1024)S(1)} %copy-done.31, f32[4096]{0:T(1024)S(1)} %copy-done.29, bf16[4096,4608]{1,0:T(8,128)(2,1)} %param.24, bf16[1024,4608]{0,1:T(8,128)(2,1)S(1)} %pad_maximum_fusion.10.clone.4), kind=kOutput, calls=%fused_computation.94 | convolution fusion | flops 38684061696 | bytes 72392704 | tf_op jit(solution)/shard_map/qc,nc->qn/dot_general | solution.py:137
  2138.6 1144.6 %all-reduce.4.cloned.1.call-done = f32[4096,4608]{1,0:T(8,128)} async-done(((f32[4096,4608]{1,0:T(8,128)}), f32[4096,4608]{1,0:T(8,128)}) %all-reduce.4.cloned.1.call-update) | async-done | bytes 75497488 | tf_op jit(solution)/shard_map/psum | solution.py:141
  3283.2 50.2 %copy.188 = f32[4096,4608]{1,0:T(8,128)} copy(f32[4096,4608]{1,0:T(8,128)} %all-reduce.4.cloned.1.call-done) | data formatting | bytes 150994944
  3333.5 44.1 %copy.189 = f32[4096,4096]{1,0:T(8,128)} copy(f32[4096,4096]{1,0:T(8,128)} %all-reduce.6.cloned.1.call-done) | data formatting | bytes 134217728
  (238 shorter events, 602.8 us)
Async XLA Ops:
  7.2 2131.5 %all-reduce.6.cloned.1.call-start = ((), (), s32[]{:S(2)}) async-start(), calls=%async_computation.1 | async-start | bytes 134217728 | tf_op jit(solution)/shard_map/psum | solution.py:141
  394.3 11.8 collective-permute-start.1
  407.0 151.9 %collective-permute-start = (s32[1024]{0:T(1024)S(1)}, s32[1024]{0:T(1024)S(1)}, u32[]{:S(2)}, u32[]{:S(2)}) collective-permute-start(s32[1024]{0:T(1024)S(1)} %get-tuple-element.925), channel_id=1, source_target_pairs={{0,1},{1,2},{2,3},{3,0},{4,5},{5,6},{6,7},{7,4}} | collective-permute-start | bytes 12296 | tf_op jit(solution)/shard_map/while/body/eval_jaxpr/ppermute | solution.py:94
  571.5 150.0 %collective-permute-start = (s32[1024]{0:T(1024)S(1)}, s32[1024]{0:T(1024)S(1)}, u32[]{:S(2)}, u32[]{:S(2)}) collective-permute-start(s32[1024]{0:T(1024)S(1)} %get-tuple-element.925), channel_id=1, source_target_pairs={{0,1},{1,2},{2,3},{3,0},{4,5},{5,6},{6,7},{7,4}} | collective-permute-start | bytes 12296 | tf_op jit(solution)/shard_map/while/body/eval_jaxpr/ppermute | solution.py:94
  571.6 155.5 %collective-permute-start.2 = (bf16[1024,2,128]{2,0,1:T(8,128)(2,1)}, bf16[1024,2,128]{2,0,1:T(8,128)(2,1)S(1)}, u32[]{:S(2)}, u32[]{:S(2)}) collective-permute-start(bf16[1024,2,128]{2,0,1:T(8,128)(2,1)} %get-tuple-element.924), channel_id=1, source_target_pairs={{0,1},{1,2},{2,3},{3,0},{4,5},{5,6},{6,7},{7,4}} | collective-permute-start | bytes 1572872 | tf_op jit(solution)/shard_map/while/body/eval_jaxpr/ppermute | solution.py:94
  574.1 158.7 %collective-permute-start.1 = (bf16[1024,2,128]{2,0,1:T(8,128)(2,1)S(1)}, bf16[1024,2,128]{2,0,1:T(8,128)(2,1)S(1)}, u32[]{:S(2)}, u32[]{:S(2)}) collective-permute-start(bf16[1024,2,128]{2,0,1:T(8,128)(2,1)S(1)} %get-tuple-element.923), channel_id=1, source_target_pairs={{0,1},{1,2},{2,3},{3,0},{4,5},{5,6},{6,7},{7,4}} | collective-permute-start | bytes 1572872 | tf_op jit(solution)/shard_map/while/body/eval_jaxpr/ppermute | solution.py:94
  796.9 2486.3 %all-reduce.4.cloned.1.call-start = ((), (), s32[]{:S(2)}) async-start(), calls=%async_computation | async-start | bytes 150994944 | tf_op jit(solution)/shard_map/psum | solution.py:141
  1067.1 105.1 %collective-permute-start.5 = (f32[1024,2,128]{2,0,1:T(8,128)}, f32[1024,2,128]{2,0,1:T(8,128)S(1)}, u32[]{:S(2)}, u32[]{:S(2)}) collective-permute-start(f32[1024,2,128]{2,0,1:T(8,128)} %get-tuple-element.970), channel_id=1, source_target_pairs={{0,1},{1,2},{2,3},{3,0},{4,5},{5,6},{6,7},{7,4}} | collective-permute-start | bytes 3145736 | tf_op jit(solution)/shard_map/while/body/eval_jaxpr/ppermute | solution.py:124
  1067.1 105.0 %collective-permute-start.4 = (f32[1024,2,128]{2,0,1:T(8,128)}, f32[1024,2,128]{2,0,1:T(8,128)S(1)}, u32[]{:S(2)}, u32[]{:S(2)}) collective-permute-start(f32[1024,2,128]{2,0,1:T(8,128)} %get-tuple-element.969), channel_id=1, source_target_pairs={{0,1},{1,2},{2,3},{3,0},{4,5},{5,6},{6,7},{7,4}} | collective-permute-start | bytes 3145736 | tf_op jit(solution)/shard_map/while/body/eval_jaxpr/ppermute | solution.py:124
  1069.3 68.3 %collective-permute-start.3 = (s32[1024]{0:T(1024)S(1)}, s32[1024]{0:T(1024)S(1)}, u32[]{:S(2)}, u32[]{:S(2)}) collective-permute-start(s32[1024]{0:T(1024)S(1)} %get-tuple-element.973), channel_id=1, source_target_pairs={{0,1},{1,2},{2,3},{3,0},{4,5},{5,6},{6,7},{7,4}} | collective-permute-start | bytes 12296 | tf_op jit(solution)/shard_map/while/body/eval_jaxpr/ppermute | solution.py:124
  1069.4 85.1 %collective-permute-start.7 = (bf16[1024,2,128]{2,0,1:T(8,128)(2,1)}, bf16[1024,2,128]{2,0,1:T(8,128)(2,1)S(1)}, u32[]{:S(2)}, u32[]{:S(2)}) collective-permute-start(bf16[1024,2,128]{2,0,1:T(8,128)(2,1)} %get-tuple-element.972), channel_id=1, source_target_pairs={{0,1},{1,2},{2,3},{3,0},{4,5},{5,6},{6,7},{7,4}} | collective-permute-start | bytes 1572872 | tf_op jit(solution)/shard_map/while/body/eval_jaxpr/ppermute | solution.py:124
  1069.4 102.0 %collective-permute-start.6 = (bf16[1024,2,128]{2,0,1:T(8,128)(2,1)}, bf16[1024,2,128]{2,0,1:T(8,128)(2,1)S(1)}, u32[]{:S(2)}, u32[]{:S(2)}) collective-permute-start(bf16[1024,2,128]{2,0,1:T(8,128)(2,1)} %get-tuple-element.971), channel_id=1, source_target_pairs={{0,1},{1,2},{2,3},{3,0},{4,5},{5,6},{6,7},{7,4}} | collective-permute-start | bytes 1572872 | tf_op jit(solution)/shard_map/while/body/eval_jaxpr/ppermute | solution.py:124
  1176.4 343.9 %collective-permute-start.5 = (f32[1024,2,128]{2,0,1:T(8,128)}, f32[1024,2,128]{2,0,1:T(8,128)S(1)}, u32[]{:S(2)}, u32[]{:S(2)}) collective-permute-start(f32[1024,2,128]{2,0,1:T(8,128)} %get-tuple-element.970), channel_id=1, source_target_pairs={{0,1},{1,2},{2,3},{3,0},{4,5},{5,6},{6,7},{7,4}} | collective-permute-start | bytes 3145736 | tf_op jit(solution)/shard_map/while/body/eval_jaxpr/ppermute | solution.py:124
  1425.0 95.4 %collective-permute-start.4 = (f32[1024,2,128]{2,0,1:T(8,128)}, f32[1024,2,128]{2,0,1:T(8,128)S(1)}, u32[]{:S(2)}, u32[]{:S(2)}) collective-permute-start(f32[1024,2,128]{2,0,1:T(8,128)} %get-tuple-element.969), channel_id=1, source_target_pairs={{0,1},{1,2},{2,3},{3,0},{4,5},{5,6},{6,7},{7,4}} | collective-permute-start | bytes 3145736 | tf_op jit(solution)/shard_map/while/body/eval_jaxpr/ppermute | solution.py:124
  1427.5 58.4 %collective-permute-start.3 = (s32[1024]{0:T(1024)S(1)}, s32[1024]{0:T(1024)S(1)}, u32[]{:S(2)}, u32[]{:S(2)}) collective-permute-start(s32[1024]{0:T(1024)S(1)} %get-tuple-element.973), channel_id=1, source_target_pairs={{0,1},{1,2},{2,3},{3,0},{4,5},{5,6},{6,7},{7,4}} | collective-permute-start | bytes 12296 | tf_op jit(solution)/shard_map/while/body/eval_jaxpr/ppermute | solution.py:124
  1427.5 75.2 %collective-permute-start.7 = (bf16[1024,2,128]{2,0,1:T(8,128)(2,1)}, bf16[1024,2,128]{2,0,1:T(8,128)(2,1)S(1)}, u32[]{:S(2)}, u32[]{:S(2)}) collective-permute-start(bf16[1024,2,128]{2,0,1:T(8,128)(2,1)} %get-tuple-element.972), channel_id=1, source_target_pairs={{0,1},{1,2},{2,3},{3,0},{4,5},{5,6},{6,7},{7,4}} | collective-permute-start | bytes 1572872 | tf_op jit(solution)/shard_map/while/body/eval_jaxpr/ppermute | solution.py:124
  1427.5 92.1 %collective-permute-start.6 = (bf16[1024,2,128]{2,0,1:T(8,128)(2,1)}, bf16[1024,2,128]{2,0,1:T(8,128)(2,1)S(1)}, u32[]{:S(2)}, u32[]{:S(2)}) collective-permute-start(bf16[1024,2,128]{2,0,1:T(8,128)(2,1)} %get-tuple-element.971), channel_id=1, source_target_pairs={{0,1},{1,2},{2,3},{3,0},{4,5},{5,6},{6,7},{7,4}} | collective-permute-start | bytes 1572872 | tf_op jit(solution)/shard_map/while/body/eval_jaxpr/ppermute | solution.py:124
  1524.7 351.4 %collective-permute-start.5 = (f32[1024,2,128]{2,0,1:T(8,128)}, f32[1024,2,128]{2,0,1:T(8,128)S(1)}, u32[]{:S(2)}, u32[]{:S(2)}) collective-permute-start(f32[1024,2,128]{2,0,1:T(8,128)} %get-tuple-element.970), channel_id=1, source_target_pairs={{0,1},{1,2},{2,3},{3,0},{4,5},{5,6},{6,7},{7,4}} | collective-permute-start | bytes 3145736 | tf_op jit(solution)/shard_map/while/body/eval_jaxpr/ppermute | solution.py:124
  1534.3 341.8 %collective-permute-start.4 = (f32[1024,2,128]{2,0,1:T(8,128)}, f32[1024,2,128]{2,0,1:T(8,128)S(1)}, u32[]{:S(2)}, u32[]{:S(2)}) collective-permute-start(f32[1024,2,128]{2,0,1:T(8,128)} %get-tuple-element.969), channel_id=1, source_target_pairs={{0,1},{1,2},{2,3},{3,0},{4,5},{5,6},{6,7},{7,4}} | collective-permute-start | bytes 3145736 | tf_op jit(solution)/shard_map/while/body/eval_jaxpr/ppermute | solution.py:124
  1536.8 304.7 %collective-permute-start.3 = (s32[1024]{0:T(1024)S(1)}, s32[1024]{0:T(1024)S(1)}, u32[]{:S(2)}, u32[]{:S(2)}) collective-permute-start(s32[1024]{0:T(1024)S(1)} %get-tuple-element.973), channel_id=1, source_target_pairs={{0,1},{1,2},{2,3},{3,0},{4,5},{5,6},{6,7},{7,4}} | collective-permute-start | bytes 12296 | tf_op jit(solution)/shard_map/while/body/eval_jaxpr/ppermute | solution.py:124
  1773.3 85.1 %collective-permute-start.7 = (bf16[1024,2,128]{2,0,1:T(8,128)(2,1)}, bf16[1024,2,128]{2,0,1:T(8,128)(2,1)S(1)}, u32[]{:S(2)}, u32[]{:S(2)}) collective-permute-start(bf16[1024,2,128]{2,0,1:T(8,128)(2,1)} %get-tuple-element.972), channel_id=1, source_target_pairs={{0,1},{1,2},{2,3},{3,0},{4,5},{5,6},{6,7},{7,4}} | collective-permute-start | bytes 1572872 | tf_op jit(solution)/shard_map/while/body/eval_jaxpr/ppermute | solution.py:124
  1773.3 102.0 %collective-permute-start.6 = (bf16[1024,2,128]{2,0,1:T(8,128)(2,1)}, bf16[1024,2,128]{2,0,1:T(8,128)(2,1)S(1)}, u32[]{:S(2)}, u32[]{:S(2)}) collective-permute-start(bf16[1024,2,128]{2,0,1:T(8,128)(2,1)} %get-tuple-element.971), channel_id=1, source_target_pairs={{0,1},{1,2},{2,3},{3,0},{4,5},{5,6},{6,7},{7,4}} | collective-permute-start | bytes 1572872 | tf_op jit(solution)/shard_map/while/body/eval_jaxpr/ppermute | solution.py:124
  1882.2 57.3 %collective-permute-start.9 = (bf16[1024,2,128]{0,2,1:T(8,128)(2,1)S(1)}, bf16[1024,2,128]{0,2,1:T(8,128)(2,1)S(1)}, u32[]{:S(2)}, u32[]{:S(2)}) collective-permute-start(bf16[1024,2,128]{0,2,1:T(8,128)(2,1)S(1)} %copy.62), channel_id=1, source_target_pairs={{0,1},{1,2},{2,3},{3,0},{4,5},{5,6},{6,7},{7,4}} | collective-permute-start | bytes 1572872 | tf_op jit(solution)/shard_map/ppermute | solution.py:129
  1883.8 52.0 %collective-permute-start.8 = (f32[1024,2,128]{0,1,2:T(2,128)S(1)}, f32[1024,2,128]{0,1,2:T(2,128)}, u32[]{:S(2)}, u32[]{:S(2)}) collective-permute-start(f32[1024,2,128]{0,1,2:T(2,128)S(1)} %copy.60), channel_id=1, source_target_pairs={{0,1},{1,2},{2,3},{3,0},{4,5},{5,6},{6,7},{7,4}} | collective-permute-start | bytes 3145736 | tf_op jit(solution)/shard_map/ppermute | solution.py:129
  (41 other events, 1276.1 us)
Sparse Core Ops, SparseCore 0:
  797.0 1256.2 all-reduce.5
  2056.4 1226.8 all-reduce.3
where the time goes:
time: 3400 us; the launch traced here: 3380 us
  waiting for transfers between devices  1450 us (43%)
  starting transfers between devices  807 us (24%)
  matrix products  657 us (19%)
  local copies, waits for them, and re-layouts  275 us (8%)
  other arithmetic  159 us (5%)
    psum x2, waiting for transfers between devices, per_device(): lax.psum((grad_gain, grad_wqkv, grad_bqkv, grad_wout), 'cp')  1140 us
    ppermute x15, starting transfers between devices, bwd_turn(): lax.ppermute((k_blk, v_blk, seg_k, d_key, d_value), 'cp', shift_perm)  502 us
    ppermute x9, starting transfers between devices, fwd_turn(): k_blk, v_blk, seg_k = lax.ppermute((k_blk, v_blk, seg_k), 'cp', shift_perm)  305 us
    ppermute x15, waiting for transfers between devices, bwd_turn(): lax.ppermute((k_blk, v_blk, seg_k, d_key, d_value), 'cp', shift_perm)  280 us
    unnamed x63, local copies, waits for them, and re-layouts  158 us
    dot_general x1, matrix products, backward_update(): jnp.einsum('grqd,kgd->grqk', grad_ctx, v_blk, preferred_element_type=jnp....  79 us
    dot_general x1, matrix products, forward_update(): jnp.einsum('qgrd,kgd->grqk', q_rot, k_blk, preferred_element_type=jnp.flo...  74.5 us
  transfers between devices with their start and end apart: 28, of which 19 were waited for; matrix products, arithmetic and copies ran while one was open for 16% of the time, Pallas kernels for 0%

commit v1 on v0

v1 whole, which is shorter than its diff:
```python
import functools

import jax
import jax.numpy as jnp
from jax import lax
from jax.experimental import pallas as pl
from jax.experimental.pallas import tpu as pltpu
from jax.sharding import PartitionSpec as P

HEAD_DIM = 128
ROT_DIMS = 64
ROPE_BASE = 5000000.0
EPS_NORM = 1e-5
NEG_BIG = -1e30
LOG2E = 1.4426950408889634
BQ = 256
BK = 256
VMEM_LIMIT = 60 * 1024 * 1024


NT = (((1,), (1,)), ((), ()))
NN = (((1,), (0,)), ((), ()))
TN = (((0,), (0,)), ((), ()))


def dotf(a, b, dims):
    return lax.dot_general(a, b, dims, preferred_element_type=jnp.float32)


def pair_swap(values):
    lane = lax.broadcasted_iota(jnp.int32, values.shape, 1)
    return jnp.where(lane % 2 == 0, pltpu.roll(values, HEAD_DIM - 1, 1), pltpu.roll(values, 1, 1))


def load_rotated(q_ref, cos_ref, sin_ref, qs_ref, n_heads):
    cos_t = cos_ref[...]
    sin_t = sin_ref[...]
    for h in range(n_heads):
        val = q_ref[:, h * HEAD_DIM:(h + 1) * HEAD_DIM].astype(jnp.float32)
        qs_ref[h * BQ:(h + 1) * BQ, :] = (val * cos_t + pair_swap(val) * sin_t).astype(jnp.bfloat16)


def visible(start_row, kv, q_base):
    k_idx = kv * BK + lax.broadcasted_iota(jnp.int32, (BK, BQ), 0)
    q_idx = q_base + lax.broadcasted_iota(jnp.int32, (BK, BQ), 1)
    return (k_idx >= start_row) & (k_idx <= q_idx)


def mask_heads(s_t, start_row, kv, q_base, n_heads):
    vis = visible(start_row, kv, q_base)
    return jnp.concatenate([jnp.where(vis, s_t[:, h * BQ:(h + 1) * BQ], NEG_BIG) for h in range(n_heads)], axis=1)


def fwd_kernel(n_heads, sc_ref, q_ref, cos_ref, sin_ref, start_ref, k_ref, vt_ref,
               ctx_ref, lse_ref, qs_ref, acc_ref):
    i = pl.program_id(0)
    q_base = sc_ref[0] + i * BQ
    lo = sc_ref[1 + 2 * i]
    full_lo = sc_ref[2 + 2 * i]
    diag = q_base // BK
    scale = HEAD_DIM ** -0.5 * LOG2E
    load_rotated(q_ref, cos_ref, sin_ref, qs_ref, n_heads)
    start_row = start_ref[...]
    acc_ref[...] = jnp.zeros_like(acc_ref)

    def step(masked, kv, carry):
        m_run, l_run = carry
        k_off = pl.multiple_of(kv * BK, BK)
        s_t = dotf(k_ref[pl.ds(k_off, BK), :], qs_ref[...], NT) * scale
        if masked:
            s_t = mask_heads(s_t, start_row, kv, q_base, n_heads)
        m_new = jnp.maximum(m_run, jnp.max(s_t, axis=0, keepdims=True))
        p_t = jnp.exp2(s_t - m_new)
        rescale = jnp.exp2(m_run - m_new)
        l_new = l_run * rescale + jnp.sum(p_t, axis=0, keepdims=True)
        acc_ref[...] = acc_ref[...] * rescale + dotf(vt_ref[:, pl.ds(k_off, BK)], p_t.astype(jnp.bfloat16), NN)
        return m_new, l_new

    carry = (jnp.full((1, n_heads * BQ), NEG_BIG, jnp.float32), jnp.zeros((1, n_heads * BQ), jnp.float32))
    carry = lax.fori_loop(lo, full_lo, functools.partial(step, True), carry)
    carry = lax.fori_loop(full_lo, diag, functools.partial(step, False), carry)
    m_run, l_run = step(True, diag, carry)
    lse = m_run + jnp.log2(l_run)
    for h in range(n_heads):
        span = slice(h * BQ, (h + 1) * BQ)
        o_t = acc_ref[:, span] / l_run[:, span]
        ctx_ref[:, h * HEAD_DIM:(h + 1) * HEAD_DIM] = o_t.T.astype(jnp.bfloat16)
        lse_ref[h:h + 1, :] = lse[:, span]


def bwd_kernel(n_heads, sc_ref, q_ref, do_ref, ctx_ref, lse_ref, cos_ref, sin_ref, start_ref,
               k_ref, kt_ref, v_ref, dq_ref, dk_ref, dv_ref, qs_ref, ds_ref, rd_ref, dqt_ref):
    i = pl.program_id(0)
    q_base = sc_ref[0] + i * BQ
    lo = sc_ref[1 + 2 * i]
    full_lo = sc_ref[2 + 2 * i]
    diag = q_base // BK
    factor = HEAD_DIM ** -0.5
    scale = factor * LOG2E

    @pl.when(i == 0)
    def _():
        dk_ref[...] = jnp.zeros_like(dk_ref)
        dv_ref[...] = jnp.zeros_like(dv_ref)

    load_rotated(q_ref, cos_ref, sin_ref, qs_ref, n_heads)
    for h in range(n_heads):
        cols = slice(h * HEAD_DIM, (h + 1) * HEAD_DIM)
        do_h = do_ref[:, cols]
        ds_ref[h * BQ:(h + 1) * BQ, :] = do_h
        prod = do_h.astype(jnp.float32) * ctx_ref[:, cols].astype(jnp.float32)
        span = slice(h * BQ, (h + 1) * BQ)
        rd_ref[0:1, span] = jnp.sum(prod.T, axis=0, keepdims=True)
        rd_ref[1:2, span] = lse_ref[h:h + 1, :]
    start_row = start_ref[...]
    cos_t = cos_ref[...]
    sin_t = sin_ref[...]
    dqt_ref[...] = jnp.zeros_like(dqt_ref)
    row_dot = rd_ref[0:1, :]
    log_norm = rd_ref[1:2, :]

    def step(masked, kv, _):
        k_off = pl.multiple_of(kv * BK, BK)
        keys = pl.ds(k_off, BK)
        s_t = dotf(k_ref[keys, :], qs_ref[...], NT) * scale
        if masked:
            s_t = mask_heads(s_t, start_row, kv, q_base, n_heads)
        p_t = jnp.exp2(s_t - log_norm)
        g_t = (p_t * (dotf(v_ref[keys, :], ds_ref[...], NT) - row_dot)).astype(jnp.bfloat16)
        dqt_ref[...] += dotf(kt_ref[:, keys], g_t, NN)
        dv_ref[keys, :] += dotf(p_t.astype(jnp.bfloat16), ds_ref[...], NN)
        dk_ref[keys, :] += dotf(g_t, qs_ref[...], NN)
        return 0

    lax.fori_loop(lo, full_lo, functools.partial(step, True), 0)
    lax.fori_loop(full_lo, diag, functools.partial(step, False), 0)
    step(True, diag, 0)
    for h in range(n_heads):
        dq_h = dqt_ref[:, h * BQ:(h + 1) * BQ].T * factor
        dq_ref[:, h * HEAD_DIM:(h + 1) * HEAD_DIM] = (dq_h * cos_t - pair_swap(dq_h) * sin_t).astype(jnp.bfloat16)


def attn_cost(n_rows, width, n_dots):
    return pl.CostEstimate(flops=int(n_dots * 4 * n_rows * 1400 * width), bytes_accessed=3 * n_rows * width * 2,
                           transcendentals=0)


def attention_fwd(scal, q_pre, cos_t, sin_t, start_row, k_all, vt_all):
    n_rows, width = q_pre.shape
    n_heads = width // HEAD_DIM
    n_keys = k_all.shape[0]
    row_blk = lambda i, sc: (i, 0)
    lane_blk = lambda i, sc: (0, i)
    whole = lambda i, sc: (0, 0)
    return pl.pallas_call(
        functools.partial(fwd_kernel, n_heads),
        grid_spec=pltpu.PrefetchScalarGridSpec(
            num_scalar_prefetch=1, grid=(n_rows // BQ,),
            in_specs=[pl.BlockSpec((BQ, width), row_blk), pl.BlockSpec((BQ, HEAD_DIM), row_blk),
                      pl.BlockSpec((BQ, HEAD_DIM), row_blk), pl.BlockSpec((1, BQ), lane_blk),
                      pl.BlockSpec((n_keys, HEAD_DIM), whole), pl.BlockSpec((HEAD_DIM, n_keys), whole)],
            out_specs=[pl.BlockSpec((BQ, width), row_blk), pl.BlockSpec((n_heads, BQ), lane_blk)],
            scratch_shapes=[pltpu.VMEM((n_heads * BQ, HEAD_DIM), jnp.bfloat16),
                            pltpu.VMEM((HEAD_DIM, n_heads * BQ), jnp.float32)]),
        out_shape=[jax.ShapeDtypeStruct((n_rows, width), jnp.bfloat16), jax.ShapeDtypeStruct((n_heads, n_rows), jnp.float32)],
        compiler_params=pltpu.CompilerParams(dimension_semantics=("arbitrary",), vmem_limit_bytes=VMEM_LIMIT),
        cost_estimate=attn_cost(n_rows, width, 1), name="attn_fwd",
    )(scal, q_pre, cos_t, sin_t, start_row, k_all, vt_all)


def attention_bwd(scal, q_pre, grad_ctx, ctx, lse, cos_t, sin_t, start_row, k_all, kt_all, v_all):
    n_rows, width = q_pre.shape
    n_heads = width // HEAD_DIM
    n_keys = k_all.shape[0]
    row_blk = lambda i, sc: (i, 0)
    lane_blk = lambda i, sc: (0, i)
    whole = lambda i, sc: (0, 0)
    wide = pl.BlockSpec((BQ, width), row_blk)
    kv_spec = pl.BlockSpec((n_keys, HEAD_DIM), whole)
    return pl.pallas_call(
        functools.partial(bwd_kernel, n_heads),
        grid_spec=pltpu.PrefetchScalarGridSpec(
            num_scalar_prefetch=1, grid=(n_rows // BQ,),
            in_specs=[wide, wide, wide, pl.BlockSpec((n_heads, BQ), lane_blk), pl.BlockSpec((BQ, HEAD_DIM), row_blk),
                      pl.BlockSpec((BQ, HEAD_DIM), row_blk), pl.BlockSpec((1, BQ), lane_blk),
                      kv_spec, pl.BlockSpec((HEAD_DIM, n_keys), whole), kv_spec],
            out_specs=[wide, kv_spec, kv_spec],
            scratch_shapes=[pltpu.VMEM((n_heads * BQ, HEAD_DIM), jnp.bfloat16),
                            pltpu.VMEM((n_heads * BQ, HEAD_DIM), jnp.bfloat16),
                            pltpu.VMEM((2, n_heads * BQ), jnp.float32),
                            pltpu.VMEM((HEAD_DIM, n_heads * BQ), jnp.float32)]),
        out_shape=[jax.ShapeDtypeStruct((n_rows, width), jnp.bfloat16)] + [jax.ShapeDtypeStruct((n_keys, HEAD_DIM), jnp.float32)] * 2,
        compiler_params=pltpu.CompilerParams(dimension_semantics=("arbitrary",), vmem_limit_bytes=VMEM_LIMIT),
        cost_estimate=attn_cost(n_rows, width, 2.5), name="attn_bwd",
    )(scal, q_pre, grad_ctx, ctx, lse, cos_t, sin_t, start_row, k_all, kt_all, v_all)


def wgrad_kernel(col_step, n_prev, n_out, sc_ref, a0_ref, a1_ref, b0_ref, b1_ref, *refs):
    out_refs = refs[-n_out:]
    width = out_refs[0].shape[1]

    def cols(j, _):
        span = pl.ds(pl.multiple_of(j * col_step, col_step), col_step)
        total = dotf(a0_ref[...], b0_ref[:, span], TN) + dotf(a1_ref[...], b1_ref[:, span], TN)
        if n_prev:
            total = refs[0][:, span] + total
        for out in out_refs:
            out[:, span] = total
        return 0

    lax.fori_loop(0, width // col_step, cols, 0)


def weight_grad(a_pair, b_pair, prev, place, full, col0, n_dim, bm, bn, col_step):
    n_tok, m_dim = a_pair[0].shape
    blk0 = col0 // bn
    a_spec = pl.BlockSpec((n_tok, bm), lambda n, m, sc: (0, m))
    b_spec = pl.BlockSpec((n_tok, bn), lambda n, m, sc: (0, n + blk0))
    in_specs = [a_spec] * 2 + [b_spec] * 2
    args = [*a_pair, *b_pair]
    if prev is not None:
        in_specs.append(pl.BlockSpec((bm, bn), lambda n, m, sc: (m, n + blk0)))
        args.append(prev)
    out_specs = [pl.BlockSpec((bm, bn), lambda n, m, sc: (m, n))]
    out_shape = [jax.ShapeDtypeStruct((m_dim, n_dim), jnp.float32)]
    aliases = {}
    if full is not None:
        shape = full if isinstance(full, tuple) else full.shape
        out_specs.append(pl.BlockSpec((bm, bn), lambda n, m, sc: (sc[0] + m, sc[1] + n)))
        out_shape.append(jax.ShapeDtypeStruct(shape, jnp.float32))
        if not isinstance(full, tuple):
            in_specs.append(pl.BlockSpec(memory_space=pl.ANY))
            args.append(full)
            aliases = {len(args): 1}
    return pl.pallas_call(
        functools.partial(wgrad_kernel, col_step, prev is not None, len(out_shape)),
        grid_spec=pltpu.PrefetchScalarGridSpec(num_scalar_prefetch=1, grid=(n_dim // bn, m_dim // bm),
                                               in_specs=in_specs, out_specs=out_specs),
        out_shape=out_shape, input_output_aliases=aliases,
        compiler_params=pltpu.CompilerParams(dimension_semantics=("arbitrary", "arbitrary"), vmem_limit_bytes=VMEM_LIMIT),
        cost_estimate=pl.CostEstimate(flops=4 * n_tok * m_dim * n_dim, transcendentals=0,
                                      bytes_accessed=m_dim * n_dim * 8 + 4 * n_tok * (m_dim + n_dim)),
    )(place, *args)


def place_kernel(sc_ref, src_ref, full_ref, out_ref):
    out_ref[...] = src_ref[...]


def place_block(full, block, place, bm, bn):
    m_dim, n_dim = block.shape
    return pl.pallas_call(
        place_kernel,
        grid_spec=pltpu.PrefetchScalarGridSpec(
            num_scalar_prefetch=1, grid=(m_dim // bm, n_dim // bn),
            in_specs=[pl.BlockSpec((bm, bn), lambda m, n, sc: (m, n)), pl.BlockSpec(memory_space=pl.ANY)],
            out_specs=pl.BlockSpec((bm, bn), lambda m, n, sc: (sc[0] + m, sc[1] + n))),
        out_shape=jax.ShapeDtypeStruct(full.shape, full.dtype),
        input_output_aliases={2: 0},
        compiler_params=pltpu.CompilerParams(dimension_semantics=("arbitrary", "arbitrary"), vmem_limit_bytes=VMEM_LIMIT),
        cost_estimate=pl.CostEstimate(flops=0, transcendentals=0, bytes_accessed=8 * m_dim * n_dim),
    )(place, block, full)


def swap_lanes(values):
    lane = lax.broadcasted_iota(jnp.int32, values.shape, values.ndim - 1)
    return jnp.where(lane % 2 == 0, jnp.roll(values, -1, axis=-1), jnp.roll(values, 1, axis=-1))


def solution(mesh):
    core_swap = [(0, 1), (1, 0), (2, 3), (3, 2)]
    chip_swap = [(0, 2), (2, 0), (1, 3), (3, 1)]

    def to_core(val):
        return lax.ppermute(val, 'cp', core_swap)

    def to_chip(val):
        return lax.ppermute(val, 'cp', chip_swap)

    def to_later(val):
        return lax.ppermute(val, 'cp', [(0, 2), (1, 3)])

    def to_earlier(val):
        return lax.ppermute(val, 'cp', [(2, 0), (3, 1)])

    def layer(hidden, seg_id, doc_pos, norm_gain, w_qkv, b_qkv, w_out, grad_out):
        n_rows, hid_width = hidden.shape
        att_width = w_out.shape[0]
        half = att_width // 2
        idx = lax.axis_index('cp')
        core = idx % 2
        chip = idx // 2
        chunk_ids = (idx, idx ^ 1, idx ^ 2, idx ^ 3)

        pos_all = lax.all_gather(doc_pos, 'cp', axis=0, tiled=True)
        hidden, grad_out, pos_all = lax.optimization_barrier((hidden, grad_out, pos_all))

        go_rm = to_chip(grad_out)
        hid_f32 = hidden.astype(jnp.float32)
        inv_rms = lax.rsqrt(jnp.mean(hid_f32 * hid_f32, axis=-1, keepdims=True) + EPS_NORM)
        x_hat = hid_f32 * inv_rms
        gain_f32 = norm_gain.astype(jnp.float32)
        normed = (x_hat * gain_f32).astype(jnp.bfloat16)
        normed_p = to_core(normed)
        go_p = to_core(grad_out)

        n_seq = pos_all.shape[0]
        starts = jnp.arange(n_seq, dtype=jnp.int32) - pos_all
        lane = jnp.arange(HEAD_DIM)
        exponent = -((lane // 2) * 2).astype(jnp.float32) / ROT_DIMS
        inv_freq = ROPE_BASE ** exponent
        angles = pos_all.astype(jnp.float32)[:, None] * inv_freq[None, :]
        turned = (lane < ROT_DIMS)[None, :]
        cos_all = jnp.where(turned, jnp.cos(angles), 1.0)
        sin_all = jnp.where(turned, jnp.sin(angles) * jnp.where(lane % 2 == 0, -1.0, 1.0)[None, :], 0.0)

        def chunk_of(arr, g, axis=0):
            return lax.dynamic_slice_in_dim(arr, g * n_rows, n_rows, axis)

        cos_c = [chunk_of(cos_all, g) for g in chunk_ids]
        sin_c = [chunk_of(sin_all, g) for g in chunk_ids]
        start_c = [chunk_of(starts, g) for g in chunk_ids]
        scal_c = []
        for g, st in zip(chunk_ids, start_c):
            diag = (g * n_rows) // BK + jnp.arange(n_rows // BQ, dtype=jnp.int32) * (BQ // BK)
            lo = st[::BQ] // BK
            full_lo = jnp.minimum((st[BQ - 1::BQ] + BK - 1) // BK, diag)
            lo = jnp.minimum(lo, full_lo)
            scal_c.append(jnp.concatenate([(g * n_rows)[None], jnp.stack([lo, full_lo], axis=1).reshape(-1)]).astype(jnp.int32))
        row_c = [st[None, :] for st in start_c]

        wq = lax.dynamic_slice(w_qkv, (0, core * half), (hid_width, half))
        wk = lax.dynamic_slice(w_qkv, (0, att_width + core * HEAD_DIM), (hid_width, HEAD_DIM))
        wv = lax.dynamic_slice(w_qkv, (0, att_width + (2 + core) * HEAD_DIM), (hid_width, HEAD_DIM))
        wkv = jnp.concatenate([wk, wv], axis=1)
        b_f32 = b_qkv.astype(jnp.float32)
        bq = lax.dynamic_slice(b_f32, (core * half,), (half,))
        bkv = jnp.concatenate([lax.dynamic_slice(b_f32, (att_width + core * HEAD_DIM,), (HEAD_DIM,)),
                               lax.dynamic_slice(b_f32, (att_width + (2 + core) * HEAD_DIM,), (HEAD_DIM,))])
        wo = lax.dynamic_slice(w_out, (core * half, 0), (half, hid_width))

        def project(act, wgt, bias):
            return (jnp.dot(act, wgt, preferred_element_type=jnp.float32) + bias).astype(jnp.bfloat16)

        def project_kv(act, i):
            kv = project(act, wkv, bkv)
            k_f32 = kv[:, :HEAD_DIM].astype(jnp.float32)
            k_rot = (k_f32 * cos_c[i] + swap_lanes(k_f32) * sin_c[i]).astype(jnp.bfloat16)
            return jnp.concatenate([k_rot, kv[:, HEAD_DIM:]], axis=1)

        kv_m = project_kv(normed, 0)
        kv_rm = to_later(kv_m)
        kv_p = project_kv(normed_p, 1)
        kv_rp = to_later(kv_p)
        norm_sent, kv_m, kv_p = lax.optimization_barrier((normed, kv_m, kv_p))
        norm_rm = to_chip(norm_sent)
        q_m = project(normed, wq, bq)
        q_p = project(normed_p, wq, bq)

        def grad_context(go):
            return lax.dot_general(go, wo, NT, preferred_element_type=jnp.float32).astype(jnp.bfloat16)

        gctx_m, gctx_p = grad_context(grad_out), grad_context(go_p)
        kv_rm, kv_rp, q_m, q_p, gctx_m, gctx_p = lax.optimization_barrier((kv_rm, kv_rp, q_m, q_p, gctx_m, gctx_p))
        kv_all = jnp.zeros((n_seq, 2 * HEAD_DIM), jnp.bfloat16)
        for g, kv in zip(chunk_ids, (kv_m, kv_p, kv_rm, kv_rp)):
            kv_all = lax.dynamic_update_slice(kv_all, kv, (g * n_rows, 0))
        k_all, v_all = kv_all[:, :HEAD_DIM], kv_all[:, HEAD_DIM:]
        kt_all, vt_all = k_all.T, v_all.T

        def forward(i, q):
            return attention_fwd(scal_c[i], q, cos_c[i], sin_c[i], row_c[i], k_all, vt_all)

        def backward(i, q, ctx, lse, gctx):
            return attention_bwd(scal_c[i], q, gctx, ctx, lse, cos_c[i], sin_c[i], row_c[i], k_all, kt_all, v_all)

        ctx_m, lse_m = forward(0, q_m)
        ctx_rm = to_chip(ctx_m)
        q_p, ctx_m = lax.optimization_barrier((q_p, ctx_m))
        ctx_p, lse_p = forward(1, q_p)
        ctx_rp = to_chip(ctx_p)
        ctx_o = to_core(ctx_p)
        q_m, ctx_m, ctx_p = lax.optimization_barrier((q_m, ctx_m, ctx_p))
        dq_m, dk_m, dv_m = backward(0, q_m, ctx_m, lse_m, gctx_m)
        q_p, dq_m = lax.optimization_barrier((q_p, dq_m))
        dq_p, dk_p, dv_p = backward(1, q_p, ctx_p, lse_p, gctx_p)

        two = 2 * n_rows
        d_kv = jnp.concatenate([dk_m + dk_p, dv_m + dv_p], axis=1)
        d_kv_mine = lax.dynamic_slice(d_kv, (chip * two, 0), (two, 2 * HEAD_DIM))
        d_kv_sent = lax.dynamic_slice(d_kv, ((1 - chip) * two, 0), (two, 2 * HEAD_DIM))
        d_kv_got = to_earlier(d_kv_sent)
        d_kv_sent, go_rm, norm_rm = lax.optimization_barrier((d_kv_sent, go_rm, norm_rm))
        dq_rm = to_chip(dq_m)
        dq_rp = to_chip(dq_p)
        dq_o = to_core(dq_p)
        go_rp = to_core(go_rm)
        norm_rp = to_core(norm_rm)

        no_place = jnp.zeros((2,), jnp.int32)
        bm, bn = 512, 2048
        wout_own, = weight_grad((ctx_m, ctx_p), (grad_out, go_p), None, no_place, None, 0, hid_width, bm, bn, 512)
        wq_own, = weight_grad((normed, normed_p), (dq_m, dq_p), None, no_place, None, 0, half, bm, bn, 512)

        def both_halves(mine, other):
            first = jnp.where(core == 0, mine, other)
            second = jnp.where(core == 0, other, mine)
            return jnp.concatenate([first, second], axis=-1)

        ctx_full = both_halves(ctx_m, ctx_o)
        y_out = (hid_f32 + jnp.dot(ctx_full, w_out, preferred_element_type=jnp.float32)).astype(jnp.bfloat16)

        ctx_rm, ctx_rp, go_rp, y_out, wq_own = lax.optimization_barrier((ctx_rm, ctx_rp, go_rp, y_out, wq_own))
        mine_o = jnp.stack([core * (half // bm), jnp.int32(0)]).astype(jnp.int32)
        other_o = jnp.stack([(1 - core) * (half // bm), jnp.int32(0)]).astype(jnp.int32)
        wout_half, wout_full = weight_grad((ctx_rm, ctx_rp), (go_rm, go_rp), wout_own, mine_o, (att_width, hid_width), 0, hid_width,
                                           bm, bn // 2, 512)
        wout_other = to_core(wout_half)

        d_kv = d_kv_mine + d_kv_got
        d_key = d_kv[:, :HEAD_DIM] * (HEAD_DIM ** -0.5)
        cos_k = lax.dynamic_slice(cos_all, (chip * two, 0), (two, HEAD_DIM))
        sin_k = lax.dynamic_slice(sin_all, (chip * two, 0), (two, HEAD_DIM))
        d_key = d_key * cos_k - swap_lanes(d_key) * sin_k
        d_kv = jnp.concatenate([d_key, d_kv[:, HEAD_DIM:]], axis=1).astype(jnp.bfloat16)
        d_kv_r = to_chip(d_kv)

        def pair_of(arr):
            return [lax.dynamic_slice(arr, (c * n_rows, 0), (n_rows, 2 * HEAD_DIM)) for c in (core, 1 - core)]

        dkv_m, dkv_p = pair_of(d_kv)
        dkv_o = to_core(dkv_p)
        grad_qkv = jnp.concatenate([both_halves(dq_m, dq_o),
                                    both_halves(dkv_m[:, :HEAD_DIM], dkv_o[:, :HEAD_DIM]),
                                    both_halves(dkv_m[:, HEAD_DIM:], dkv_o[:, HEAD_DIM:])], axis=1)
        grad_normed = lax.dot_general(grad_qkv, w_qkv, NT, preferred_element_type=jnp.float32)
        grad_gain = jnp.sum(grad_normed * x_hat, axis=0)
        scaled = grad_normed * gain_f32
        grad_hidden = (grad_out.astype(jnp.float32) + inv_rms * (scaled - x_hat * jnp.mean(scaled * x_hat, axis=-1, keepdims=True))).astype(jnp.bfloat16)
        kv_own, = weight_grad((normed, normed_p), (dkv_m, dkv_p), None, no_place, None, 0, 2 * HEAD_DIM, 1024, 2 * HEAD_DIM, 256)
        grad_wout = place_block(wout_full, wout_other, other_o, 512, 2048)

        def col_sums(first, second):
            return jnp.sum(first.astype(jnp.float32), axis=0) + jnp.sum(second.astype(jnp.float32), axis=0)

        own_sums = jnp.concatenate([col_sums(dq_m, dq_p), col_sums(dkv_m, dkv_p)])
        (dq_rm, dq_rp, norm_rm, norm_rp, grad_hidden, kv_own, own_sums, grad_wout) = lax.optimization_barrier(
            (dq_rm, dq_rp, norm_rm, norm_rp, grad_hidden, kv_own, own_sums, grad_wout))
        n_rem = (norm_rm, norm_rp)
        bn_q = half // 2
        grad_wqkv, sent = w_qkv.shape, []
        for part in range(2):
            mine_q = jnp.stack([jnp.int32(0), core * 2 + part]).astype(jnp.int32)
            other_q = jnp.stack([jnp.int32(0), (1 - core) * 2 + part]).astype(jnp.int32)
            got, grad_wqkv = weight_grad(n_rem, (dq_rm, dq_rp), wq_own, mine_q, grad_wqkv, part * bn_q, bn_q, bm, bn_q, 512)
            sent.append((to_core(got), other_q))
        d_kv_r, grad_wqkv = lax.optimization_barrier((d_kv_r, grad_wqkv))
        dkv_r = pair_of(d_kv_r)
        kv_half, = weight_grad(n_rem, dkv_r, kv_own, no_place, None, 0, 2 * HEAD_DIM, 1024, 2 * HEAD_DIM, 256)
        kv_other = to_core(kv_half)
        for got, other_q in sent:
            grad_wqkv = place_block(grad_wqkv, got, other_q, 512, bn_q)
        kv_cols = jnp.concatenate([both_halves(kv_half[:, :HEAD_DIM], kv_other[:, :HEAD_DIM]),
                                   both_halves(kv_half[:, HEAD_DIM:], kv_other[:, HEAD_DIM:])], axis=1)
        grad_wqkv = lax.dynamic_update_slice(grad_wqkv, kv_cols, (0, att_width))

        b_half = own_sums + to_chip(own_sums)
        b_other = to_core(b_half)
        grad_bqkv = jnp.concatenate([both_halves(b_half[:half], b_other[:half]),
                                     both_halves(b_half[half:half + HEAD_DIM], b_other[half:half + HEAD_DIM]),
                                     both_halves(b_half[half + HEAD_DIM:], b_other[half + HEAD_DIM:])])
        grad_gain = grad_gain + to_core(grad_gain)
        grad_gain = grad_gain + to_chip(grad_gain)
        return y_out, grad_hidden, grad_gain, grad_wqkv, grad_bqkv, grad_wout

    act_spec = P(('dp', 'cp'), None)
    row_spec = P(('dp', 'cp'))
    return jax.shard_map(layer, mesh=mesh,
                         in_specs=(act_spec, row_spec, row_spec, P(), P(), P(), P(), act_spec),
                         out_specs=(act_spec, act_spec, P('dp'), P('dp', None), P('dp'), P('dp', None)),
                         check_vma=False)
```

time: 3400 us -> 1110 us (0.33)
  the two profiles are of different devices: /device:TPU:0 before, /device:TPU:4 now
where the time goes in v1:
time: 1110 us
  Pallas kernels  451 us (41%)
  matrix products  198 us (18%)
  waiting for transfers between devices  191 us (17%)
  starting transfers between devices  154 us (14%)
  other arithmetic  91.8 us (8%)
  local copies, waits for them, and re-layouts  12.3 us (1%)
    pallas_call x7, Pallas kernels, weight_grad(): pl.pallas_call(functools.partial(wgrad_kernel, col_step, prev is not None...  250 us
    ppermute x9, starting transfers between devices, to_chip(): return lax.ppermute(val, 'cp', chip_swap)  147 us
    pallas_call x2, Pallas kernels, attention_bwd(): pl.pallas_call(functools.partial(bwd_kernel, n_heads), grid_spec=pltpu.Pr...  91.5 us
    ppermute x9, waiting for transfers between devices, to_chip(): return lax.ppermute(val, 'cp', chip_swap)  88.3 us
    dot_general x4, matrix products, project(): jnp.dot(act, wgt, preferred_element_type=jnp.float32) + bias  60.9 us
    ppermute x2, waiting for transfers between devices, to_later(): return lax.ppermute(val, 'cp', [(0, 2), (1, 3)])  58.2 us
    pallas_call x2, Pallas kernels, attention_fwd(): pl.pallas_call(functools.partial(fwd_kernel, n_heads), grid_spec=pltpu.Pr...  57.3 us
    pallas_call x3, Pallas kernels, place_block(): pl.pallas_call(place_kernel, grid_spec=pltpu.PrefetchScalarGridSpec(num_s...  52.2 us
  transfers between devices with their start and end apart: 25, of which 7 were waited for; matrix products, arithmetic and copies ran while one was open for 27% of the time, Pallas kernels for 31%

profile of v1, /device:TPU:4, one launch (start us, length us, event | category | flops | bytes accessed | tf_op | source)
XLA Modules:
  0.0 1106.8 jit_solution(15112135604219696303)
XLA Ops:
  25.3 24.1 %fusion.31.do_ref = bf16[1024,2048]{1,0:T(8,128)(2,1)} fusion(bf16[1024,4096]{1,0:T(8,128)(2,1)} %b0_ref, bf16[4096,4096]{1,0:T(8,128)(2,1)} %param.13, s32[]{:T(128)S(6)} %select_n.250), kind=kOutput, calls=%fused_computation.41 | convolution fusion | flops 17181966336 | bytes 29360132 | tf_op jit(solution)/shard_map/dot_general | solution.py:361
  58.1 24.1 %add_convert_fusion.1.q_ref = bf16[1024,2048]{1,0:T(8,128)(2,1)} fusion(f32[2048]{0:T(1024)S(1)} %dynamic_slice.73, bf16[1024,4096]{1,0:T(8,128)(2,1)} %fusion.4.a0_ref, bf16[4096,4608]{1,0:T(8,128)(2,1)} %param.11, s32[]{:T(128)S(6)} %select_n.249), kind=kOutput, calls=%fused_computation.32 | convolution fusion | flops 17184063488 | bytes 29368324 | tf_op jit(solution)/shard_map/dot_general | solution.py:343
  105.7 23.8 %add_convert_fusion.q_ref = bf16[1024,2048]{1,0:T(8,128)(2,1)} fusion(f32[2048]{0:T(1024)S(1)} %dynamic_slice.73, bf16[1024,4096]{1,0:T(8,128)(2,1)} %collective-permute-done.1.a1_ref, bf16[4096,4608]{1,0:T(8,128)(2,1)} %param.11, s32[]{:T(128)S(6)} %select_n.249), kind=kOutput, calls=%fused_computation.31 | convolution fusion | flops 17184063488 | bytes 29368324 | tf_op jit(solution)/shard_map/dot_general | solution.py:343
  129.6 23.8 %fusion.34.do_ref = bf16[1024,2048]{1,0:T(8,128)(2,1)} fusion(bf16[1024,4096]{1,0:T(8,128)(2,1)} %collective-permute-done.3.b1_ref, bf16[4096,4096]{1,0:T(8,128)(2,1)} %param.13, s32[]{:T(128)S(6)} %select_n.250), kind=kOutput, calls=%fused_computation.42 | convolution fusion | flops 17181966336 | bytes 29360132 | tf_op jit(solution)/shard_map/dot_general | solution.py:361
  153.6 47.0 %collective-permute-done = bf16[1024,256]{1,0:T(8,128)(2,1)S(1)} collective-permute-done((bf16[1024,256]{1,0:T(8,128)(2,1)S(1)}, bf16[1024,256]{1,0:T(8,128)(2,1)S(1)}, u32[]{:S(2)}, u32[]{:S(2)}) %collective-permute-start) | collective-permute-done | bytes 524320 | tf_op jit(solution)/shard_map/ppermute | solution.py:281
  215.1 27.6 %attn_fwd.2 = (bf16[1024,2048]{1,0:T(8,128)(2,1)}, f32[16,1024]{1,0:T(8,128)}) custom-call(s32[9]{0:T(128)} %pad_add_fusion.8.sc_ref, bf16[1024,2048]{1,0:T(8,128)(2,1)} %add_convert_fusion.1.q_ref, f32[1024,128]{1,0:T(8,128)} %get-tuple-element.136.cos_ref, f32[1024,128]{1,0:T(8,128)} %get-tuple-element.135.sin_ref, s32[1,1024]{1,0:T(1,128)} %bitcast.35, ...), custom_call_target="tpu_custom_call" | custom-call | flops 11744051200 | bytes 12582912 | tf_op jit(solution)/shard_map/attn_fwd/pallas_call | solution.py:155
  242.8 17.5 %collective-permute-start.4 = (bf16[1024,2048]{1,0:T(8,128)(2,1)}, bf16[1024,2048]{1,0:T(8,128)(2,1)}, u32[]{:S(2)}, u32[]{:S(2)}) collective-permute-start(bf16[1024,2048]{1,0:T(8,128)(2,1)} %get-tuple-element.73.ctx_ref.a0_ref), channel_id=1, source_target_pairs={{0,2},{2,0},{1,3},{3,1},{4,6},{6,4},{5,7},{7,5}} | collective-permute-start | bytes 12582920 | tf_op jit(solution)/shard_map/ppermute | solution.py:278
  260.3 29.6 %attn_fwd.3 = (bf16[1024,2048]{1,0:T(8,128)(2,1)}, f32[16,1024]{1,0:T(8,128)}) custom-call(s32[9]{0:T(128)} %pad_add_fusion.9.sc_ref, bf16[1024,2048]{1,0:T(8,128)(2,1)} %add_convert_fusion.q_ref, f32[1024,128]{1,0:T(8,128)} %get-tuple-element.119.cos_ref, f32[1024,128]{1,0:T(8,128)} %get-tuple-element.120.sin_ref, s32[1,1024]{1,0:T(1,128)} %bitcast.33, ...), custom_call_target="tpu_custom_call" | custom-call | flops 11744051200 | bytes 12582912 | tf_op jit(solution)/shard_map/attn_fwd/pallas_call | solution.py:155
  290.0 43.0 %collective-permute-start.5 = (bf16[1024,2048]{1,0:T(8,128)(2,1)}, bf16[1024,2048]{1,0:T(8,128)(2,1)}, u32[]{:S(2)}, u32[]{:S(2)}) collective-permute-start(bf16[1024,2048]{1,0:T(8,128)(2,1)} %get-tuple-element.79.ctx_ref.a1_ref), channel_id=1, source_target_pairs={{0,2},{2,0},{1,3},{3,1},{4,6},{6,4},{5,7},{7,5}} | collective-permute-start | bytes 12582920 | tf_op jit(solution)/shard_map/ppermute | solution.py:278
  334.8 48.3 %shard_map.120.refs_0_ = f32[2048,4096]{1,0:T(8,128)} custom-call(s32[2]{0:T(128)} %broadcast_15_sc_ref.2.sc_ref, bf16[1024,2048]{1,0:T(8,128)(2,1)} %get-tuple-element.73.ctx_ref.a0_ref, bf16[1024,2048]{1,0:T(8,128)(2,1)} %get-tuple-element.79.ctx_ref.a1_ref, bf16[1024,4096]{1,0:T(8,128)(2,1)} %b0_ref, bf16[1024,4096]{1,0:T(8,128)(2,1)} %collective-permute-done.3.b1_ref), custom_call_target="tpu_custom_call" | custom-call | flops 34359738368 | bytes 92274688 | tf_op jit(solution)/shard_map/pallas_call | solution.py:235
  383.1 43.3 %attn_bwd.2 = (bf16[1024,2048]{1,0:T(8,128)(2,1)}, f32[4096,128]{1,0:T(8,128)}, f32[4096,128]{1,0:T(8,128)}) custom-call(s32[9]{0:T(128)} %pad_add_fusion.8.sc_ref, bf16[1024,2048]{1,0:T(8,128)(2,1)} %add_convert_fusion.1.q_ref, bf16[1024,2048]{1,0:T(8,128)(2,1)} %fusion.31.do_ref, bf16[1024,2048]{1,0:T(8,128)(2,1)} %get-tuple-element.73.ctx_ref.a0_ref, ...), custom_call_target="tpu_custom_call" | custom-call | flops 29360128000 | bytes 12582912 | tf_op jit(solution)/shard_map/attn_bwd/pallas_call | solution.py:180
  426.5 48.2 %attn_bwd.3 = (bf16[1024,2048]{1,0:T(8,128)(2,1)}, f32[4096,128]{1,0:T(8,128)}, f32[4096,128]{1,0:T(8,128)}) custom-call(s32[9]{0:T(128)} %pad_add_fusion.9.sc_ref, bf16[1024,2048]{1,0:T(8,128)(2,1)} %add_convert_fusion.q_ref, bf16[1024,2048]{1,0:T(8,128)(2,1)} %fusion.34.do_ref, bf16[1024,2048]{1,0:T(8,128)(2,1)} %get-tuple-element.79.ctx_ref.a1_ref, ...), custom_call_target="tpu_custom_call" | custom-call | flops 29360128000 | bytes 12582912 | tf_op jit(solution)/shard_map/attn_bwd/pallas_call | solution.py:180
  481.7 47.9 %shard_map.118.refs_0_ = f32[4096,2048]{1,0:T(8,128)} custom-call(s32[2]{0:T(128)} %broadcast_15_sc_ref.2.sc_ref, bf16[1024,4096]{1,0:T(8,128)(2,1)} %fusion.4.a0_ref, bf16[1024,4096]{1,0:T(8,128)(2,1)} %collective-permute-done.1.a1_ref, bf16[1024,2048]{1,0:T(8,128)(2,1)} %get-tuple-element.86.b0_ref, bf16[1024,2048]{1,0:T(8,128)(2,1)} %get-tuple-element.87.b1_ref), custom_call_target="tpu_custom_call" | custom-call | flops 34359738368 | bytes 92274688 | tf_op jit(solution)/shard_map/pallas_call | solution.py:235
  533.9 39.8 %fusion.12 = bf16[1024,4096]{1,0:T(8,128)(2,1)} fusion(bf16[1024,4096]{1,0:T(8,128)(2,1)} %param.8, bf16[4096,4096]{1,0:T(8,128)(2,1)} %param.13, bf16[1024,2048]{1,0:T(8,128)(2,1)S(1)} %get-tuple-element.133, bf16[1024,2048]{1,0:T(8,128)(2,1)S(1)} %get-tuple-element.132), kind=kOutput, calls=%fused_computation.15 | convolution fusion | flops 34389098496 | bytes 58720256 | tf_op jit(solution)/shard_map/dot_general | solution.py:411
  573.7 65.5 %shard_map.121 = (f32[2048,4096]{1,0:T(8,128)}, f32[4096,4096]{1,0:T(8,128)}) custom-call(s32[2]{0:T(128)} %pad_add_fusion.6.sc_ref, bf16[1024,2048]{1,0:T(8,128)(2,1)} %collective-permute-done.4.a0_ref, bf16[1024,2048]{1,0:T(8,128)(2,1)} %collective-permute-done.5.a1_ref, bf16[1024,4096]{1,0:T(8,128)(2,1)} %collective-permute-done.6.b0_ref, ...), custom_call_target="tpu_custom_call" | custom-call | flops 34359738368 | bytes 92274688 | tf_op jit(solution)/shard_map/pallas_call | solution.py:235
  642.4 84.3 %collective-permute-start.10 = (bf16[1024,2048]{1,0:T(8,128)(2,1)}, bf16[1024,2048]{1,0:T(8,128)(2,1)}, u32[]{:S(2)}, u32[]{:S(2)}) collective-permute-start(bf16[1024,2048]{1,0:T(8,128)(2,1)} %get-tuple-element.86.b0_ref), channel_id=1, source_target_pairs={{0,2},{2,0},{1,3},{3,1},{4,6},{6,4},{5,7},{7,5}} | collective-permute-start | bytes 12582920 | tf_op jit(solution)/shard_map/ppermute | solution.py:278
  732.4 37.9 %collective-permute-done.14 = f32[2048,256]{1,0:T(8,128)} collective-permute-done((f32[2048,256]{1,0:T(8,128)}, f32[2048,256]{1,0:T(8,128)}, u32[]{:S(2)}, u32[]{:S(2)}) %collective-permute-start.14) | collective-permute-done | bytes 2097184 | tf_op jit(solution)/shard_map/ppermute | solution.py:284
  804.5 49.6 %fusion.10 = (f32[4096]{0:T(1024)S(1)}, f32[1024]{0:T(1024)S(1)}, f32[1024,4096]{1,0:T(8,128)}) fusion(bf16[1024,4096]{1,0:T(8,128)(2,1)S(1)} %bitcast.30, f32[1024]{0:T(1024)S(1)} %copy-done.20, f32[4096]{0:T(1024)S(1)} %copy-done.17, bf16[1024,4608]{1,0:T(8,128)(2,1)} %select_dynamic-update-slice_fusion.2, bf16[4096,4608]{1,0:T(8,128)(2,1)} %param.11), kind=kOutput, calls=%fused_computation.13 | convolution fusion | flops 38684061696 | bytes 72392704 | tf_op jit(solution)/shard_map/dot_general | solution.py:436
  866.3 23.2 %shard_map.122 = f32[4096,4096]{1,0:T(8,128)} custom-call(s32[2]{0:T(128)} %pad_add_fusion.7.sc_ref, f32[2048,4096]{1,0:T(8,128)} %collective-permute-done.16.src_ref, f32[4096,4096]{1,0:T(8,128)} %get-tuple-element.94.full_ref), custom_call_target="tpu_custom_call", output_to_operand_aliasing={{}: (2, {})} | custom-call | bytes 67108864 | tf_op jit(solution)/shard_map/pallas_call | solution.py:252
  889.6 60.3 %collective-permute-done.11.b1_ref = bf16[1024,2048]{1,0:T(8,128)(2,1)} collective-permute-done((bf16[1024,2048]{1,0:T(8,128)(2,1)}, bf16[1024,2048]{1,0:T(8,128)(2,1)}, u32[]{:S(2)}, u32[]{:S(2)}) %collective-permute-start.11) | collective-permute-done | bytes 4194336 | tf_op jit(solution)/shard_map/ppermute | solution.py:278
  949.9 32.0 %shard_map.123 = (f32[4096,1024]{1,0:T(8,128)}, f32[4096,4608]{1,0:T(8,128)}) custom-call(s32[2]{0:T(128)} %get-tuple-element.174.sc_ref, bf16[1024,4096]{1,0:T(8,128)(2,1)} %collective-permute-done.7.a0_ref, bf16[1024,4096]{1,0:T(8,128)(2,1)} %collective-permute-done.12.a1_ref, bf16[1024,2048]{1,0:T(8,128)(2,1)} %collective-permute-done.10.b0_ref, ...), custom_call_target="tpu_custom_call" | custom-call | flops 17179869184 | bytes 54525952 | tf_op jit(solution)/shard_map/pallas_call | solution.py:235
  981.9 32.3 %shard_map.124 = (f32[4096,1024]{1,0:T(8,128)}, f32[4096,4608]{1,0:T(8,128)}) custom-call(s32[2]{0:T(128)} %get-tuple-element.175.sc_ref, bf16[1024,4096]{1,0:T(8,128)(2,1)} %collective-permute-done.7.a0_ref, bf16[1024,4096]{1,0:T(8,128)(2,1)} %collective-permute-done.12.a1_ref, ...), custom_call_target="tpu_custom_call", output_to_operand_aliasing={{1}: (6, {})} | custom-call | flops 17179869184 | bytes 54525952 | tf_op jit(solution)/shard_map/pallas_call | solution.py:235
  1014.8 25.1 %collective-permute-done.21 = bf16[2048,256]{1,0:T(8,128)(2,1)S(1)} collective-permute-done((bf16[2048,256]{1,0:T(8,128)(2,1)S(1)}, bf16[2048,256]{1,0:T(8,128)(2,1)S(1)}, u32[]{:S(2)}, u32[]{:S(2)}) %collective-permute-start.21) | collective-permute-done | bytes 1048608 | tf_op jit(solution)/shard_map/ppermute | solution.py:278
  1072.1 14.5 %shard_map.125.full_ref = f32[4096,4608]{1,0:T(8,128)} custom-call(s32[2]{0:T(128)} %pad_add_fusion.2.sc_ref, f32[4096,1024]{1,0:T(8,128)} %collective-permute-done.20.src_ref, f32[4096,4608]{1,0:T(8,128)} %get-tuple-element.105.full_ref), custom_call_target="tpu_custom_call", output_to_operand_aliasing={{}: (2, {})} | custom-call | bytes 33554432 | tf_op jit(solution)/shard_map/pallas_call | solution.py:252
  (209 shorter events, 192.4 us)
Async XLA Ops:
  7.2 122.3 %collective-permute-start.3 = (bf16[1024,4096]{1,0:T(8,128)(2,1)}, bf16[1024,4096]{1,0:T(8,128)(2,1)}, u32[]{:S(2)}, u32[]{:S(2)}) collective-permute-start(bf16[1024,4096]{1,0:T(8,128)(2,1)} %b0_ref), channel_id=1, source_target_pairs={{0,1},{1,0},{2,3},{3,2},{4,5},{5,4},{6,7},{7,6}} | collective-permute-start | bytes 25165832 | tf_op jit(solution)/shard_map/ppermute | solution.py:275
  7.3 526.1 %collective-permute-start.6 = (bf16[1024,4096]{1,0:T(8,128)(2,1)}, bf16[1024,4096]{1,0:T(8,128)(2,1)}, u32[]{:S(2)}, u32[]{:S(2)}) collective-permute-start(bf16[1024,4096]{1,0:T(8,128)(2,1)} %b0_ref), channel_id=1, source_target_pairs={{0,2},{2,0},{1,3},{3,1},{4,6},{6,4},{5,7},{7,5}} | collective-permute-start | bytes 25165832 | tf_op jit(solution)/shard_map/ppermute | solution.py:278
  24.6 66.9 %collective-permute-start.1 = (bf16[1024,4096]{1,0:T(8,128)(2,1)}, bf16[1024,4096]{1,0:T(8,128)(2,1)}, u32[]{:S(2)}, u32[]{:S(2)}) collective-permute-start(bf16[1024,4096]{1,0:T(8,128)(2,1)} %fusion.4.a0_ref), channel_id=1, source_target_pairs={{0,1},{1,0},{2,3},{3,2},{4,5},{5,4},{6,7},{7,6}} | collective-permute-start | bytes 25165832 | tf_op jit(solution)/shard_map/ppermute | solution.py:275
  101.2 99.4 %collective-permute-start = (bf16[1024,256]{1,0:T(8,128)(2,1)S(1)}, bf16[1024,256]{1,0:T(8,128)(2,1)S(1)}, u32[]{:S(2)}, u32[]{:S(2)}) collective-permute-start(bf16[1024,256]{1,0:T(8,128)(2,1)S(1)} %pad_maximum_fusion.12), channel_id=1, source_target_pairs={{0,2},{1,3},{4,6},{5,7}} | collective-permute-start | bytes 1572872 | tf_op jit(solution)/shard_map/ppermute | solution.py:281
  104.4 107.5 %collective-permute-start.2 = (bf16[1024,256]{1,0:T(8,128)(2,1)S(1)}, bf16[1024,256]{1,0:T(8,128)(2,1)S(1)}, u32[]{:S(2)}, u32[]{:S(2)}) collective-permute-start(bf16[1024,256]{1,0:T(8,128)(2,1)S(1)} %pad_maximum_fusion.13), channel_id=1, source_target_pairs={{0,2},{1,3},{4,6},{5,7}} | collective-permute-start | bytes 1572872 | tf_op jit(solution)/shard_map/ppermute | solution.py:281
  105.7 427.7 %collective-permute-start.7 = (bf16[1024,4096]{1,0:T(8,128)(2,1)}, bf16[1024,4096]{1,0:T(8,128)(2,1)}, u32[]{:S(2)}, u32[]{:S(2)}) collective-permute-start(bf16[1024,4096]{1,0:T(8,128)(2,1)} %fusion.4.a0_ref), channel_id=1, source_target_pairs={{0,2},{2,0},{1,3},{3,1},{4,6},{6,4},{5,7},{7,5}} | collective-permute-start | bytes 25165832 | tf_op jit(solution)/shard_map/ppermute | solution.py:278
  242.8 330.9 %collective-permute-start.4 = (bf16[1024,2048]{1,0:T(8,128)(2,1)}, bf16[1024,2048]{1,0:T(8,128)(2,1)}, u32[]{:S(2)}, u32[]{:S(2)}) collective-permute-start(bf16[1024,2048]{1,0:T(8,128)(2,1)} %get-tuple-element.73.ctx_ref.a0_ref), channel_id=1, source_target_pairs={{0,2},{2,0},{1,3},{3,1},{4,6},{6,4},{5,7},{7,5}} | collective-permute-start | bytes 12582920 | tf_op jit(solution)/shard_map/ppermute | solution.py:278
  290.0 283.7 %collective-permute-start.5 = (bf16[1024,2048]{1,0:T(8,128)(2,1)}, bf16[1024,2048]{1,0:T(8,128)(2,1)}, u32[]{:S(2)}, u32[]{:S(2)}) collective-permute-start(bf16[1024,2048]{1,0:T(8,128)(2,1)} %get-tuple-element.79.ctx_ref.a1_ref), channel_id=1, source_target_pairs={{0,2},{2,0},{1,3},{3,1},{4,6},{6,4},{5,7},{7,5}} | collective-permute-start | bytes 12582920 | tf_op jit(solution)/shard_map/ppermute | solution.py:278
  333.0 196.6 %collective-permute-start.9 = (bf16[1024,2048]{1,0:T(8,128)(2,1)}, bf16[1024,2048]{1,0:T(8,128)(2,1)}, u32[]{:S(2)}, u32[]{:S(2)}) collective-permute-start(bf16[1024,2048]{1,0:T(8,128)(2,1)} %get-tuple-element.79.ctx_ref.a1_ref), channel_id=1, source_target_pairs={{0,1},{1,0},{2,3},{3,2},{4,5},{5,4},{6,7},{7,6}} | collective-permute-start | bytes 12582920 | tf_op jit(solution)/shard_map/ppermute | solution.py:275
  533.4 40.3 %collective-permute-start.8 = (bf16[1024,4096]{1,0:T(8,128)(2,1)}, bf16[1024,4096]{1,0:T(8,128)(2,1)}, u32[]{:S(2)}, u32[]{:S(2)}) collective-permute-start(bf16[1024,4096]{1,0:T(8,128)(2,1)} %collective-permute-done.6.b0_ref), channel_id=1, source_target_pairs={{0,1},{1,0},{2,3},{3,2},{4,5},{5,4},{6,7},{7,6}} | collective-permute-start | bytes 25165832 | tf_op jit(solution)/shard_map/ppermute | solution.py:275
  639.2 227.1 %collective-permute-start.16 = (f32[2048,4096]{1,0:T(8,128)}, f32[2048,4096]{1,0:T(8,128)}, u32[]{:S(2)}, u32[]{:S(2)}) collective-permute-start(f32[2048,4096]{1,0:T(8,128)} %get-tuple-element.93), channel_id=1, source_target_pairs={{0,1},{1,0},{2,3},{3,2},{4,5},{5,4},{6,7},{7,6}} | collective-permute-start | bytes 100663304 | tf_op jit(solution)/shard_map/ppermute | solution.py:275
  639.2 131.1 %collective-permute-start.14 = (f32[2048,256]{1,0:T(8,128)}, f32[2048,256]{1,0:T(8,128)}, u32[]{:S(2)}, u32[]{:S(2)}) collective-permute-start(f32[2048,256]{1,0:T(8,128)} %fusion.42), channel_id=1, source_target_pairs={{2,0},{3,1},{6,4},{7,5}} | collective-permute-start | bytes 6291464 | tf_op jit(solution)/shard_map/ppermute | solution.py:284
  640.7 147.4 %collective-permute-start.13 = (bf16[1024,2048]{1,0:T(8,128)(2,1)}, bf16[1024,2048]{1,0:T(8,128)(2,1)}, u32[]{:S(2)}, u32[]{:S(2)}) collective-permute-start(bf16[1024,2048]{1,0:T(8,128)(2,1)} %get-tuple-element.87.b1_ref), channel_id=1, source_target_pairs={{0,1},{1,0},{2,3},{3,2},{4,5},{5,4},{6,7},{7,6}} | collective-permute-start | bytes 12582920 | tf_op jit(solution)/shard_map/ppermute | solution.py:275
  642.4 247.2 %collective-permute-start.10 = (bf16[1024,2048]{1,0:T(8,128)(2,1)}, bf16[1024,2048]{1,0:T(8,128)(2,1)}, u32[]{:S(2)}, u32[]{:S(2)}) collective-permute-start(bf16[1024,2048]{1,0:T(8,128)(2,1)} %get-tuple-element.86.b0_ref), channel_id=1, source_target_pairs={{0,2},{2,0},{1,3},{3,1},{4,6},{6,4},{5,7},{7,5}} | collective-permute-start | bytes 12582920 | tf_op jit(solution)/shard_map/ppermute | solution.py:278
  726.7 223.2 %collective-permute-start.11 = (bf16[1024,2048]{1,0:T(8,128)(2,1)}, bf16[1024,2048]{1,0:T(8,128)(2,1)}, u32[]{:S(2)}, u32[]{:S(2)}) collective-permute-start(bf16[1024,2048]{1,0:T(8,128)(2,1)} %get-tuple-element.87.b1_ref), channel_id=1, source_target_pairs={{0,2},{2,0},{1,3},{3,1},{4,6},{6,4},{5,7},{7,5}} | collective-permute-start | bytes 12582920 | tf_op jit(solution)/shard_map/ppermute | solution.py:278
  775.6 25.5 %collective-permute-start.15 = (bf16[1024,256]{1,0:T(8,128)(2,1)S(1)}, bf16[1024,256]{1,0:T(8,128)(2,1)S(1)}, u32[]{:S(2)}, u32[]{:S(2)}) collective-permute-start(bf16[1024,256]{1,0:T(8,128)(2,1)S(1)} %get-tuple-element.144.b1_ref), channel_id=1, source_target_pairs={{0,1},{1,0},{2,3},{3,2},{4,5},{5,4},{6,7},{7,6}} | collective-permute-start | bytes 1572872 | tf_op jit(solution)/shard_map/ppermute | solution.py:275
  804.4 145.5 %collective-permute-start.12 = (bf16[1024,4096]{1,0:T(8,128)(2,1)}, bf16[1024,4096]{1,0:T(8,128)(2,1)}, u32[]{:S(2)}, u32[]{:S(2)}) collective-permute-start(bf16[1024,4096]{1,0:T(8,128)(2,1)} %collective-permute-done.7.a0_ref), channel_id=1, source_target_pairs={{0,1},{1,0},{2,3},{3,2},{4,5},{5,4},{6,7},{7,6}} | collective-permute-start | bytes 25165832 | tf_op jit(solution)/shard_map/ppermute | solution.py:275
  981.9 90.2 %collective-permute-start.20 = (f32[4096,1024]{1,0:T(8,128)}, f32[4096,1024]{1,0:T(8,128)}, u32[]{:S(2)}, u32[]{:S(2)}) collective-permute-start(f32[4096,1024]{1,0:T(8,128)} %get-tuple-element.103), channel_id=1, source_target_pairs={{0,1},{1,0},{2,3},{3,2},{4,5},{5,4},{6,7},{7,6}} | collective-permute-start | bytes 50331656 | tf_op jit(solution)/shard_map/ppermute | solution.py:275
  1014.2 72.4 %collective-permute-start.19 = (f32[4096,1024]{1,0:T(8,128)}, f32[4096,1024]{1,0:T(8,128)}, u32[]{:S(2)}, u32[]{:S(2)}) collective-permute-start(f32[4096,1024]{1,0:T(8,128)} %get-tuple-element.102), channel_id=1, source_target_pairs={{0,1},{1,0},{2,3},{3,2},{4,5},{5,4},{6,7},{7,6}} | collective-permute-start | bytes 50331656 | tf_op jit(solution)/shard_map/ppermute | solution.py:275
  1014.8 25.1 %collective-permute-start.21 = (bf16[2048,256]{1,0:T(8,128)(2,1)S(1)}, bf16[2048,256]{1,0:T(8,128)(2,1)S(1)}, u32[]{:S(2)}, u32[]{:S(2)}) collective-permute-start(bf16[2048,256]{1,0:T(8,128)(2,1)S(1)} %pad_maximum_fusion.3), channel_id=1, source_target_pairs={{0,2},{2,0},{1,3},{3,1},{4,6},{6,4},{5,7},{7,5}} | collective-permute-start | bytes 3145736 | tf_op jit(solution)/shard_map/ppermute | solution.py:278
  1053.8 11.9 %collective-permute-start.22 = (f32[4096,256]{1,0:T(8,128)}, f32[4096,256]{1,0:T(8,128)}, u32[]{:S(2)}, u32[]{:S(2)}) collective-permute-start(f32[4096,256]{1,0:T(8,128)} %shard_map.127), channel_id=1, source_target_pairs={{0,1},{1,0},{2,3},{3,2},{4,5},{5,4},{6,7},{7,6}} | collective-permute-start | bytes 12582920 | tf_op jit(solution)/shard_map/ppermute | solution.py:275
  1053.8 7.5 collective-permute-start.17
  1054.3 7.3 collective-permute-start.23
  1061.6 4.1 collective-permute-start.24
  (36 other events, 917.6 us)

commit v2 on v1

--- a/solution.py
+++ b/solution.py
@@ -195,13 +195,16 @@
     )(scal, q_pre, grad_ctx, ctx, lse, cos_t, sin_t, start_row, k_all, kt_all, v_all)
 
 
-def wgrad_kernel(col_step, n_prev, n_out, sc_ref, a0_ref, a1_ref, b0_ref, b1_ref, *refs):
+def wgrad_kernel(col_step, n_prev, n_out, sc_ref, *refs):
+    a_refs, b_refs, refs = refs[:4], refs[4:8], refs[8:]
     out_refs = refs[-n_out:]
     width = out_refs[0].shape[1]
 
     def cols(j, _):
         span = pl.ds(pl.multiple_of(j * col_step, col_step), col_step)
-        total = dotf(a0_ref[...], b0_ref[:, span], TN) + dotf(a1_ref[...], b1_ref[:, span], TN)
+        total = dotf(a_refs[0][...], b_refs[0][:, span], TN)
+        for a_ref, b_ref in zip(a_refs[1:], b_refs[1:]):
+            total += dotf(a_ref[...], b_ref[:, span], TN)
         if n_prev:
             total = refs[0][:, span] + total
         for out in out_refs:
@@ -214,10 +217,22 @@
 def weight_grad(a_pair, b_pair, prev, place, full, col0, n_dim, bm, bn, col_step):
     n_tok, m_dim = a_pair[0].shape
     blk0 = col0 // bn
-    a_spec = pl.BlockSpec((n_tok, bm), lambda n, m, sc: (0, m))
-    b_spec = pl.BlockSpec((n_tok, bn), lambda n, m, sc: (0, n + blk0))
-    in_specs = [a_spec] * 2 + [b_spec] * 2
-    args = [*a_pair, *b_pair]
+
+    def piece(val, side):
+        first, second = val if isinstance(val, tuple) else (val, val)
+        shape = (n_tok // 2, bm if side == 0 else bn)
+        specs = []
+        for row in (0, 0 if isinstance(val, tuple) else 1):
+            index = (lambda n, m, sc, row=row: (row, m)) if side == 0 else (lambda n, m, sc, row=row: (row, n + blk0))
+            specs.append(pl.BlockSpec(shape, index))
+        return [first, second], specs
+
+    in_specs, args = [], []
+    for side, pair in enumerate((a_pair, b_pair)):
+        for val in pair:
+            arrs, specs = piece(val, side)
+            args += arrs
+            in_specs += specs
     if prev is not None:
         in_specs.append(pl.BlockSpec((bm, bn), lambda n, m, sc: (m, n + blk0)))
         args.append(prev)
@@ -295,7 +310,7 @@
         pos_all = lax.all_gather(doc_pos, 'cp', axis=0, tiled=True)
         hidden, grad_out, pos_all = lax.optimization_barrier((hidden, grad_out, pos_all))
 
-        go_rm = to_chip(grad_out)
+        go_ra = to_chip(grad_out[:n_rows // 2])
         hid_f32 = hidden.astype(jnp.float32)
         inv_rms = lax.rsqrt(jnp.mean(hid_f32 * hid_f32, axis=-1, keepdims=True) + EPS_NORM)
         x_hat = hid_f32 * inv_rms
@@ -352,8 +367,8 @@
         kv_rm = to_later(kv_m)
         kv_p = project_kv(normed_p, 1)
         kv_rp = to_later(kv_p)
-        norm_sent, kv_m, kv_p = lax.optimization_barrier((normed, kv_m, kv_p))
-        norm_rm = to_chip(norm_sent)
+        go_rb = to_chip(grad_out[n_rows // 2:])
+        norm_rm = to_chip(normed)
         q_m = project(normed, wq, bq)
         q_p = project(normed_p, wq, bq)
 
@@ -390,11 +405,12 @@
         d_kv_mine = lax.dynamic_slice(d_kv, (chip * two, 0), (two, 2 * HEAD_DIM))
         d_kv_sent = lax.dynamic_slice(d_kv, ((1 - chip) * two, 0), (two, 2 * HEAD_DIM))
         d_kv_got = to_earlier(d_kv_sent)
-        d_kv_sent, go_rm, norm_rm = lax.optimization_barrier((d_kv_sent, go_rm, norm_rm))
+        d_kv_sent, go_ra, go_rb, norm_rm = lax.optimization_barrier((d_kv_sent, go_ra, go_rb, norm_rm))
         dq_rm = to_chip(dq_m)
         dq_rp = to_chip(dq_p)
         dq_o = to_core(dq_p)
-        go_rp = to_core(go_rm)
+        go_rm = (go_ra, go_rb)
+        go_rp = (to_core(go_ra), to_core(go_rb))
         norm_rp = to_core(norm_rm)
 
         no_place = jnp.zeros((2,), jnp.int32)
@@ -414,7 +430,8 @@
         mine_o = jnp.stack([core * (half // bm), jnp.int32(0)]).astype(jnp.int32)
         other_o = jnp.stack([(1 - core) * (half // bm), jnp.int32(0)]).astype(jnp.int32)
         wout_half, wout_full = weight_grad((ctx_rm, ctx_rp), (go_rm, go_rp), wout_own, mine_o, (att_width, hid_width), 0, hid_width,
-                                           bm, bn // 2, 512)
+                                           bm, bn, 512)
+        wout_half, d_kv_got = lax.optimization_barrier((wout_half, d_kv_got))
         wout_other = to_core(wout_half)
 
         d_kv = d_kv_mine + d_kv_got
@@ -454,10 +471,11 @@
             other_q = jnp.stack([jnp.int32(0), (1 - core) * 2 + part]).astype(jnp.int32)
             got, grad_wqkv = weight_grad(n_rem, (dq_rm, dq_rp), wq_own, mine_q, grad_wqkv, part * bn_q, bn_q, bm, bn_q, 512)
             sent.append((to_core(got), other_q))
-        d_kv_r, grad_wqkv = lax.optimization_barrier((d_kv_r, grad_wqkv))
-        dkv_r = pair_of(d_kv_r)
-        kv_half, = weight_grad(n_rem, dkv_r, kv_own, no_place, None, 0, 2 * HEAD_DIM, 1024, 2 * HEAD_DIM, 256)
-        kv_other = to_core(kv_half)
+            if part == 0:
+                d_kv_r, grad_wqkv = lax.optimization_barrier((d_kv_r, grad_wqkv))
+                dkv_r = pair_of(d_kv_r)
+                kv_half, = weight_grad(n_rem, dkv_r, kv_own, no_place, None, 0, 2 * HEAD_DIM, 1024, 2 * HEAD_DIM, 256)
+                kv_other = to_core(kv_half)
         for got, other_q in sent:
             grad_wqkv = place_block(grad_wqkv, got, other_q, 512, bn_q)
         kv_cols = jnp.concatenate([both_halves(kv_half[:, :HEAD_DIM], kv_other[:, :HEAD_DIM]),

time: 1110 us -> 1240 us (1.12)
  the two profiles are of different devices: /device:TPU:4 before, /device:TPU:6 now
where the time goes in v2:
time: 1240 us
  Pallas kernels  585 us (47%)
  waiting for transfers between devices  328 us (26%)
  matrix products  194 us (16%)
  other arithmetic  90.2 us (7%)
  local copies, waits for them, and re-layouts  18.8 us (2%)
  starting transfers between devices  14.1 us (1%)
    ppermute x2, waiting for transfers between devices, to_later(): return lax.ppermute(val, 'cp', [(0, 2), (1, 3)])  251 us
    pallas_call x7, Pallas kernels, weight_grad(): pl.pallas_call(functools.partial(wgrad_kernel, col_step, prev is not None...  244 us
    pallas_call x2, Pallas kernels, attention_bwd(): pl.pallas_call(functools.partial(bwd_kernel, n_heads), grid_spec=pltpu.Pr...  174 us
    pallas_call x2, Pallas kernels, attention_fwd(): pl.pallas_call(functools.partial(fwd_kernel, n_heads), grid_spec=pltpu.Pr...  115 us
    dot_general x4, matrix products, project(): jnp.dot(act, wgt, preferred_element_type=jnp.float32) + bias  58.2 us
    ppermute x14, waiting for transfers between devices, to_core(): return lax.ppermute(val, 'cp', core_swap)  56.2 us
    pallas_call x3, Pallas kernels, place_block(): pl.pallas_call(place_kernel, grid_spec=pltpu.PrefetchScalarGridSpec(num_s...  52.2 us
    dot_general x1, matrix products, layer(): lax.dot_general(grad_qkv, w_qkv, NT, preferred_element_type=jnp.float32)  48.5 us
  transfers between devices with their start and end apart: 27, of which 6 were waited for; matrix products, arithmetic and copies ran while one was open for 23% of the time, Pallas kernels for 46%

profile of v2, /device:TPU:6, one launch (start us, length us, event | category | flops | bytes accessed | tf_op | source)
XLA Modules:
  0.0 1237.8 jit_solution(12065270735196246828)
XLA Ops:
  42.8 24.0 %fusion.31.do_ref = bf16[1024,2048]{1,0:T(8,128)(2,1)} fusion(bf16[1024,4096]{1,0:T(8,128)(2,1)} %refs_5_, bf16[4096,4096]{1,0:T(8,128)(2,1)} %param.13, s32[]{:T(128)S(6)} %select_n.250), kind=kOutput, calls=%fused_computation.41 | convolution fusion | flops 17181966336 | bytes 29360132 | tf_op jit(solution)/shard_map/dot_general | solution.py:376
  66.8 21.3 %add_convert_fusion.1.q_ref = bf16[1024,2048]{1,0:T(8,128)(2,1)} fusion(f32[2048]{0:T(1024)S(1)} %dynamic_slice.73, bf16[1024,4096]{1,0:T(8,128)(2,1)S(1)} %bitcast.30, bf16[4096,4608]{1,0:T(8,128)(2,1)} %param.11, s32[]{:T(128)S(6)} %select_n.249), kind=kOutput, calls=%fused_computation.32 | convolution fusion | flops 17184063488 | bytes 29368324 | tf_op jit(solution)/shard_map/dot_general | solution.py:358
  108.1 23.9 %add_convert_fusion.q_ref = bf16[1024,2048]{1,0:T(8,128)(2,1)} fusion(f32[2048]{0:T(1024)S(1)} %dynamic_slice.73, bf16[1024,4096]{1,0:T(8,128)(2,1)} %collective-permute-done.1.refs_2_.refs_3_, bf16[4096,4608]{1,0:T(8,128)(2,1)} %param.11, s32[]{:T(128)S(6)} %select_n.249), kind=kOutput, calls=%fused_computation.31 | convolution fusion | flops 17184063488 | bytes 29368324 | tf_op jit(solution)/shard_map/dot_general | solution.py:358
  133.3 23.9 %fusion.34.do_ref = bf16[1024,2048]{1,0:T(8,128)(2,1)} fusion(bf16[1024,4096]{1,0:T(8,128)(2,1)} %collective-permute-done.3.refs_6_.refs_7_, bf16[4096,4096]{1,0:T(8,128)(2,1)} %param.13, s32[]{:T(128)S(6)} %select_n.250), kind=kOutput, calls=%fused_computation.42 | convolution fusion | flops 17181966336 | bytes 29360132 | tf_op jit(solution)/shard_map/dot_general | solution.py:376
  157.1 240.6 %collective-permute-done = bf16[1024,256]{1,0:T(8,128)(2,1)S(1)} collective-permute-done((bf16[1024,256]{1,0:T(8,128)(2,1)S(1)}, bf16[1024,256]{1,0:T(8,128)(2,1)S(1)}, u32[]{:S(2)}, u32[]{:S(2)}) %collective-permute-start) | collective-permute-done | bytes 524320 | tf_op jit(solution)/shard_map/ppermute | solution.py:296
  411.3 42.5 %attn_fwd.2 = (bf16[1024,2048]{1,0:T(8,128)(2,1)}, f32[16,1024]{1,0:T(8,128)}) custom-call(s32[9]{0:T(128)} %pad_add_fusion.8.sc_ref, bf16[1024,2048]{1,0:T(8,128)(2,1)} %add_convert_fusion.1.q_ref, f32[1024,128]{1,0:T(8,128)} %get-tuple-element.140.cos_ref, f32[1024,128]{1,0:T(8,128)} %get-tuple-element.139.sin_ref, s32[1,1024]{1,0:T(1,128)} %bitcast.33, ...), custom_call_target="tpu_custom_call" | custom-call | flops 11744051200 | bytes 12582912 | tf_op jit(solution)/shard_map/attn_fwd/pallas_call | solution.py:155
  453.8 72.9 %attn_fwd.3 = (bf16[1024,2048]{1,0:T(8,128)(2,1)}, f32[16,1024]{1,0:T(8,128)}) custom-call(s32[9]{0:T(128)} %pad_add_fusion.9.sc_ref, bf16[1024,2048]{1,0:T(8,128)(2,1)} %add_convert_fusion.q_ref, f32[1024,128]{1,0:T(8,128)} %get-tuple-element.121.cos_ref, f32[1024,128]{1,0:T(8,128)} %get-tuple-element.122.sin_ref, s32[1,1024]{1,0:T(1,128)} %bitcast.31, ...), custom_call_target="tpu_custom_call" | custom-call | flops 11744051200 | bytes 12582912 | tf_op jit(solution)/shard_map/attn_fwd/pallas_call | solution.py:155
  528.0 65.7 %attn_bwd.2 = (bf16[1024,2048]{1,0:T(8,128)(2,1)}, f32[4096,128]{1,0:T(8,128)}, f32[4096,128]{1,0:T(8,128)}) custom-call(s32[9]{0:T(128)} %pad_add_fusion.8.sc_ref, bf16[1024,2048]{1,0:T(8,128)(2,1)} %add_convert_fusion.1.q_ref, bf16[1024,2048]{1,0:T(8,128)(2,1)} %fusion.31.do_ref, bf16[1024,2048]{1,0:T(8,128)(2,1)} %get-tuple-element.72.ctx_ref.refs_0_.refs_1_, ...), custom_call_target="tpu_custom_call" | custom-call | flops 29360128000 | bytes 12582912 | tf_op jit(solution)/shard_map/attn_bwd/pallas_call | solution.py:180
  593.7 108.4 %attn_bwd.3 = (bf16[1024,2048]{1,0:T(8,128)(2,1)}, f32[4096,128]{1,0:T(8,128)}, f32[4096,128]{1,0:T(8,128)}) custom-call(s32[9]{0:T(128)} %pad_add_fusion.9.sc_ref, bf16[1024,2048]{1,0:T(8,128)(2,1)} %add_convert_fusion.q_ref, bf16[1024,2048]{1,0:T(8,128)(2,1)} %fusion.34.do_ref, bf16[1024,2048]{1,0:T(8,128)(2,1)} %get-tuple-element.78.ctx_ref.refs_2_.refs_3_, ...), custom_call_target="tpu_custom_call" | custom-call | flops 29360128000 | bytes 12582912 | tf_op jit(solution)/shard_map/attn_bwd/pallas_call | solution.py:180
  713.3 48.4 %shard_map.119.refs_8_ = f32[2048,4096]{1,0:T(8,128)} custom-call(s32[2]{0:T(128)} %broadcast_15_sc_ref.2.sc_ref, bf16[1024,2048]{1,0:T(8,128)(2,1)} %get-tuple-element.72.ctx_ref.refs_0_.refs_1_, bf16[1024,2048]{1,0:T(8,128)(2,1)} %get-tuple-element.72.ctx_ref.refs_0_.refs_1_, bf16[1024,2048]{1,0:T(8,128)(2,1)} %get-tuple-element.78.ctx_ref.refs_2_.refs_3_, ...), custom_call_target="tpu_custom_call" | custom-call | flops 34359738368 | bytes 92274688 | tf_op jit(solution)/shard_map/pallas_call | solution.py:250
  761.7 48.0 %shard_map.118.refs_8_ = f32[4096,2048]{1,0:T(8,128)} custom-call(s32[2]{0:T(128)} %broadcast_15_sc_ref.2.sc_ref, bf16[1024,4096]{1,0:T(8,128)(2,1)} %fusion.4.refs_0_.refs_1_, bf16[1024,4096]{1,0:T(8,128)(2,1)} %fusion.4.refs_0_.refs_1_, bf16[1024,4096]{1,0:T(8,128)(2,1)} %collective-permute-done.1.refs_2_.refs_3_, ...), custom_call_target="tpu_custom_call" | custom-call | flops 34359738368 | bytes 92274688 | tf_op jit(solution)/shard_map/pallas_call | solution.py:250
  813.5 39.8 %fusion.12 = bf16[1024,4096]{1,0:T(8,128)(2,1)} fusion(bf16[1024,4096]{1,0:T(8,128)(2,1)} %param.8, bf16[4096,4096]{1,0:T(8,128)(2,1)} %param.13, bf16[1024,2048]{1,0:T(8,128)(2,1)S(1)} %get-tuple-element.135, bf16[1024,2048]{1,0:T(8,128)(2,1)S(1)} %get-tuple-element.134), kind=kOutput, calls=%fused_computation.15 | convolution fusion | flops 34389098496 | bytes 58720256 | tf_op jit(solution)/shard_map/dot_general | solution.py:427
  853.3 58.0 %shard_map.120 = (f32[2048,4096]{1,0:T(8,128)}, f32[4096,4096]{1,0:T(8,128)}) custom-call(s32[2]{0:T(128)} %pad_add_fusion.7.sc_ref, bf16[1024,2048]{1,0:T(8,128)(2,1)} %collective-permute-done.4.refs_0_.refs_1_, bf16[1024,2048]{1,0:T(8,128)(2,1)} %collective-permute-done.4.refs_0_.refs_1_, bf16[1024,2048]{1,0:T(8,128)(2,1)} %collective-permute-done.5.refs_2_.refs_3_, ...), custom_call_target="tpu_custom_call" | custom-call | flops 34359738368 | bytes 92274688 | tf_op jit(solution)/shard_map/pallas_call | solution.py:250
  925.6 41.4 %collective-permute-done.15 = bf16[1024,2048]{1,0:T(8,128)(2,1)} collective-permute-done((bf16[1024,2048]{1,0:T(8,128)(2,1)}, bf16[1024,2048]{1,0:T(8,128)(2,1)}, u32[]{:S(2)}, u32[]{:S(2)}) %collective-permute-start.15) | collective-permute-done | bytes 4194336 | tf_op jit(solution)/shard_map/ppermute | solution.py:290
  979.2 12.6 %shard_map.121.refs_8_ = f32[4096,256]{1,0:T(8,128)} custom-call(s32[2]{0:T(128)} %broadcast_15_sc_ref.2.sc_ref, bf16[1024,4096]{1,0:T(8,128)(2,1)} %fusion.4.refs_0_.refs_1_, bf16[1024,4096]{1,0:T(8,128)(2,1)} %fusion.4.refs_0_.refs_1_, bf16[1024,4096]{1,0:T(8,128)(2,1)} %collective-permute-done.1.refs_2_.refs_3_, ...), custom_call_target="tpu_custom_call" | custom-call | flops 4294967296 | bytes 26214400 | tf_op jit(solution)/shard_map/pallas_call | solution.py:250
  994.9 48.5 %fusion.10 = (f32[4096]{0:T(1024)S(1)}, f32[1024]{0:T(1024)S(1)}, f32[1024,4096]{1,0:T(8,128)S(1)}) fusion(bf16[1024,4096]{1,0:T(8,128)(2,1)} %param.8, f32[1024]{0:T(1024)S(1)} %copy-done.16, f32[4096]{0:T(1024)S(1)} %copy-done.13, bf16[1024,4608]{1,0:T(8,128)(2,1)} %select_dynamic-update-slice_fusion.2, bf16[4096,4608]{1,0:T(8,128)(2,1)} %param.11), kind=kOutput, calls=%fused_computation.13 | convolution fusion | flops 38684061696 | bytes 72392704 | tf_op jit(solution)/shard_map/dot_general | solution.py:453
  1055.7 23.2 %shard_map.122 = f32[4096,4096]{1,0:T(8,128)} custom-call(s32[2]{0:T(128)} %pad_add_fusion.6.sc_ref, f32[2048,4096]{1,0:T(8,128)} %collective-permute-done.18.src_ref, f32[4096,4096]{1,0:T(8,128)} %get-tuple-element.96.full_ref), custom_call_target="tpu_custom_call", output_to_operand_aliasing={{}: (2, {})} | custom-call | bytes 67108864 | tf_op jit(solution)/shard_map/pallas_call | solution.py:267
  1078.9 17.9 %collective-permute-done.13.refs_6_.refs_7_ = bf16[1024,2048]{1,0:T(8,128)(2,1)} collective-permute-done((bf16[1024,2048]{1,0:T(8,128)(2,1)}, bf16[1024,2048]{1,0:T(8,128)(2,1)}, u32[]{:S(2)}, u32[]{:S(2)}) %collective-permute-start.13) | collective-permute-done | bytes 4194336 | tf_op jit(solution)/shard_map/ppermute | solution.py:293
  1096.8 31.8 %shard_map.123 = (f32[4096,1024]{1,0:T(8,128)}, f32[4096,4608]{1,0:T(8,128)}) custom-call(s32[2]{0:T(128)} %get-tuple-element.182.sc_ref, bf16[1024,4096]{1,0:T(8,128)(2,1)} %collective-permute-done.8.refs_0_.refs_1_, bf16[1024,4096]{1,0:T(8,128)(2,1)} %collective-permute-done.8.refs_0_.refs_1_, bf16[1024,4096]{1,0:T(8,128)(2,1)} %collective-permute-done.14.refs_2_.refs_3_, ...), custom_call_target="tpu_custom_call" | custom-call | flops 17179869184 | bytes 54525952 | tf_op jit(solution)/shard_map/pallas_call | solution.py:250
  1128.7 31.9 %shard_map.124 = (f32[4096,1024]{1,0:T(8,128)}, f32[4096,4608]{1,0:T(8,128)}) custom-call(s32[2]{0:T(128)} %get-tuple-element.183.sc_ref, bf16[1024,4096]{1,0:T(8,128)(2,1)} %collective-permute-done.8.refs_0_.refs_1_, bf16[1024,4096]{1,0:T(8,128)(2,1)} %collective-permute-done.8.refs_0_.refs_1_, ...), custom_call_target="tpu_custom_call", output_to_operand_aliasing={{1}: (10, {})} | custom-call | flops 17179869184 | bytes 54525952 | tf_op jit(solution)/shard_map/pallas_call | solution.py:250
  1163.3 12.9 %shard_map.127 = f32[4096,256]{1,0:T(8,128)} custom-call(s32[2]{0:T(128)} %broadcast_15_sc_ref.2.sc_ref, bf16[1024,4096]{1,0:T(8,128)(2,1)} %collective-permute-done.8.refs_0_.refs_1_, bf16[1024,4096]{1,0:T(8,128)(2,1)} %collective-permute-done.8.refs_0_.refs_1_, bf16[1024,4096]{1,0:T(8,128)(2,1)} %collective-permute-done.14.refs_2_.refs_3_, ...), custom_call_target="tpu_custom_call" | custom-call | flops 4294967296 | bytes 26214400 | tf_op jit(solution)/shard_map/pallas_call | solution.py:250
  1177.4 14.8 %collective-permute-done.19 = f32[4096]{0:T(1024)S(1)} collective-permute-done((f32[4096]{0:T(1024)S(1)}, f32[4096]{0:T(1024)S(1)}, u32[]{:S(2)}, u32[]{:S(2)}) %collective-permute-start.19) | collective-permute-done | bytes 16416 | tf_op jit(solution)/shard_map/ppermute | solution.py:290
  1203.1 14.5 %shard_map.125.full_ref = f32[4096,4608]{1,0:T(8,128)} custom-call(s32[2]{0:T(128)} %pad_add_fusion.2.sc_ref, f32[4096,1024]{1,0:T(8,128)} %collective-permute-done.23.src_ref, f32[4096,4608]{1,0:T(8,128)} %get-tuple-element.107.full_ref), custom_call_target="tpu_custom_call", output_to_operand_aliasing={{}: (2, {})} | custom-call | bytes 33554432 | tf_op jit(solution)/shard_map/pallas_call | solution.py:267
  1217.6 14.5 %shard_map.126 = f32[4096,4608]{1,0:T(8,128)} custom-call(s32[2]{0:T(128)} %pad_add_fusion.5.sc_ref, f32[4096,1024]{1,0:T(8,128)} %collective-permute-done.22.src_ref, f32[4096,4608]{1,0:T(8,128)} %shard_map.125.full_ref), custom_call_target="tpu_custom_call", output_to_operand_aliasing={{}: (2, {})} | custom-call | bytes 33554432 | tf_op jit(solution)/shard_map/pallas_call | solution.py:267
  (199 shorter events, 155.2 us)
Async XLA Ops:
  22.8 74.0 %collective-permute-start.1 = (bf16[1024,4096]{1,0:T(8,128)(2,1)}, bf16[1024,4096]{1,0:T(8,128)(2,1)}, u32[]{:S(2)}, u32[]{:S(2)}) collective-permute-start(bf16[1024,4096]{1,0:T(8,128)(2,1)} %fusion.4.refs_0_.refs_1_), channel_id=1, source_target_pairs={{0,1},{1,0},{2,3},{3,2},{4,5},{5,4},{6,7},{7,6}} | collective-permute-start | bytes 25165832 | tf_op jit(solution)/shard_map/ppermute | solution.py:290
  23.2 689.0 %collective-permute-start.8 = (bf16[1024,4096]{1,0:T(8,128)(2,1)}, bf16[1024,4096]{1,0:T(8,128)(2,1)}, u32[]{:S(2)}, u32[]{:S(2)}) collective-permute-start(bf16[1024,4096]{1,0:T(8,128)(2,1)} %fusion.4.refs_0_.refs_1_), channel_id=1, source_target_pairs={{0,2},{2,0},{1,3},{3,1},{4,6},{6,4},{5,7},{7,5}} | collective-permute-start | bytes 25165832 | tf_op jit(solution)/shard_map/ppermute | solution.py:293
  24.1 107.8 %collective-permute-start.3 = (bf16[1024,4096]{1,0:T(8,128)(2,1)}, bf16[1024,4096]{1,0:T(8,128)(2,1)}, u32[]{:S(2)}, u32[]{:S(2)}) collective-permute-start(bf16[1024,4096]{1,0:T(8,128)(2,1)} %refs_5_), channel_id=1, source_target_pairs={{0,1},{1,0},{2,3},{3,2},{4,5},{5,4},{6,7},{7,6}} | collective-permute-start | bytes 25165832 | tf_op jit(solution)/shard_map/ppermute | solution.py:290
  30.8 678.3 %collective-permute-start.6 = (bf16[512,4096]{1,0:T(8,128)(2,1)}, bf16[512,4096]{1,0:T(8,128)(2,1)}, u32[]{:S(2)}, u32[]{:S(2)}) collective-permute-start(bf16[512,4096]{1,0:T(8,128)(2,1)} %get-tuple-element.137), channel_id=1, source_target_pairs={{0,2},{2,0},{1,3},{3,1},{4,6},{6,4},{5,7},{7,5}} | collective-permute-start | bytes 12582920 | tf_op jit(solution)/shard_map/ppermute | solution.py:293
  31.6 677.5 %collective-permute-start.7 = (bf16[512,4096]{1,0:T(8,128)(2,1)}, bf16[512,4096]{1,0:T(8,128)(2,1)}, u32[]{:S(2)}, u32[]{:S(2)}) collective-permute-start(bf16[512,4096]{1,0:T(8,128)(2,1)} %get-tuple-element.136), channel_id=1, source_target_pairs={{0,2},{2,0},{1,3},{3,1},{4,6},{6,4},{5,7},{7,5}} | collective-permute-start | bytes 12582920 | tf_op jit(solution)/shard_map/ppermute | solution.py:293
  106.7 291.0 %collective-permute-start = (bf16[1024,256]{1,0:T(8,128)(2,1)S(1)}, bf16[1024,256]{1,0:T(8,128)(2,1)S(1)}, u32[]{:S(2)}, u32[]{:S(2)}) collective-permute-start(bf16[1024,256]{1,0:T(8,128)(2,1)S(1)} %get-tuple-element.156), channel_id=1, source_target_pairs={{0,2},{1,3},{4,6},{5,7}} | collective-permute-start | bytes 1572872 | tf_op jit(solution)/shard_map/ppermute | solution.py:296
  132.0 276.1 %collective-permute-start.2 = (bf16[1024,256]{1,0:T(8,128)(2,1)S(1)}, bf16[1024,256]{1,0:T(8,128)(2,1)S(1)}, u32[]{:S(2)}, u32[]{:S(2)}) collective-permute-start(bf16[1024,256]{1,0:T(8,128)(2,1)S(1)} %get-tuple-element.154), channel_id=1, source_target_pairs={{0,2},{1,3},{4,6},{5,7}} | collective-permute-start | bytes 1572872 | tf_op jit(solution)/shard_map/ppermute | solution.py:296
  453.8 399.5 %collective-permute-start.4 = (bf16[1024,2048]{1,0:T(8,128)(2,1)}, bf16[1024,2048]{1,0:T(8,128)(2,1)}, u32[]{:S(2)}, u32[]{:S(2)}) collective-permute-start(bf16[1024,2048]{1,0:T(8,128)(2,1)} %get-tuple-element.72.ctx_ref.refs_0_.refs_1_), channel_id=1, source_target_pairs={{0,2},{2,0},{1,3},{3,1},{4,6},{6,4},{5,7},{7,5}} | collective-permute-start | bytes 12582920 | tf_op jit(solution)/shard_map/ppermute | solution.py:293
  526.7 326.6 %collective-permute-start.5 = (bf16[1024,2048]{1,0:T(8,128)(2,1)}, bf16[1024,2048]{1,0:T(8,128)(2,1)}, u32[]{:S(2)}, u32[]{:S(2)}) collective-permute-start(bf16[1024,2048]{1,0:T(8,128)(2,1)} %get-tuple-element.78.ctx_ref.refs_2_.refs_3_), channel_id=1, source_target_pairs={{0,2},{2,0},{1,3},{3,1},{4,6},{6,4},{5,7},{7,5}} | collective-permute-start | bytes 12582920 | tf_op jit(solution)/shard_map/ppermute | solution.py:293
  709.1 100.6 %collective-permute-start.11 = (bf16[1024,2048]{1,0:T(8,128)(2,1)}, bf16[1024,2048]{1,0:T(8,128)(2,1)}, u32[]{:S(2)}, u32[]{:S(2)}) collective-permute-start(bf16[1024,2048]{1,0:T(8,128)(2,1)} %get-tuple-element.78.ctx_ref.refs_2_.refs_3_), channel_id=1, source_target_pairs={{0,1},{1,0},{2,3},{3,2},{4,5},{5,4},{6,7},{7,6}} | collective-permute-start | bytes 12582920 | tf_op jit(solution)/shard_map/ppermute | solution.py:290
  709.1 202.2 %collective-permute-start.16 = (f32[2048,256]{1,0:T(8,128)}, f32[2048,256]{1,0:T(8,128)}, u32[]{:S(2)}, u32[]{:S(2)}) collective-permute-start(f32[2048,256]{1,0:T(8,128)} %fusion.42), channel_id=1, source_target_pairs={{2,0},{3,1},{6,4},{7,5}} | collective-permute-start | bytes 6291464 | tf_op jit(solution)/shard_map/ppermute | solution.py:299
  712.2 141.1 %collective-permute-start.9 = (bf16[512,4096]{1,0:T(8,128)(2,1)}, bf16[512,4096]{1,0:T(8,128)(2,1)}, u32[]{:S(2)}, u32[]{:S(2)}) collective-permute-start(bf16[512,4096]{1,0:T(8,128)(2,1)} %collective-permute-done.6.refs_4_), channel_id=1, source_target_pairs={{0,1},{1,0},{2,3},{3,2},{4,5},{5,4},{6,7},{7,6}} | collective-permute-start | bytes 12582920 | tf_op jit(solution)/shard_map/ppermute | solution.py:290
  809.7 43.6 %collective-permute-start.10 = (bf16[512,4096]{1,0:T(8,128)(2,1)}, bf16[512,4096]{1,0:T(8,128)(2,1)}, u32[]{:S(2)}, u32[]{:S(2)}) collective-permute-start(bf16[512,4096]{1,0:T(8,128)(2,1)} %collective-permute-done.7.refs_5_), channel_id=1, source_target_pairs={{0,1},{1,0},{2,3},{3,2},{4,5},{5,4},{6,7},{7,6}} | collective-permute-start | bytes 12582920 | tf_op jit(solution)/shard_map/ppermute | solution.py:290
  911.3 144.4 %collective-permute-start.18 = (f32[2048,4096]{1,0:T(8,128)}, f32[2048,4096]{1,0:T(8,128)}, u32[]{:S(2)}, u32[]{:S(2)}) collective-permute-start(f32[2048,4096]{1,0:T(8,128)} %get-tuple-element.95), channel_id=1, source_target_pairs={{0,1},{1,0},{2,3},{3,2},{4,5},{5,4},{6,7},{7,6}} | collective-permute-start | bytes 100663304 | tf_op jit(solution)/shard_map/ppermute | solution.py:290
  911.9 55.1 %collective-permute-start.15 = (bf16[1024,2048]{1,0:T(8,128)(2,1)}, bf16[1024,2048]{1,0:T(8,128)(2,1)}, u32[]{:S(2)}, u32[]{:S(2)}) collective-permute-start(bf16[1024,2048]{1,0:T(8,128)(2,1)} %get-tuple-element.86.refs_6_.refs_7_), channel_id=1, source_target_pairs={{0,1},{1,0},{2,3},{3,2},{4,5},{5,4},{6,7},{7,6}} | collective-permute-start | bytes 12582920 | tf_op jit(solution)/shard_map/ppermute | solution.py:290
  913.2 165.7 %collective-permute-start.12 = (bf16[1024,2048]{1,0:T(8,128)(2,1)}, bf16[1024,2048]{1,0:T(8,128)(2,1)}, u32[]{:S(2)}, u32[]{:S(2)}) collective-permute-start(bf16[1024,2048]{1,0:T(8,128)(2,1)} %get-tuple-element.85.refs_4_.refs_5_), channel_id=1, source_target_pairs={{0,2},{2,0},{1,3},{3,1},{4,6},{6,4},{5,7},{7,5}} | collective-permute-start | bytes 12582920 | tf_op jit(solution)/shard_map/ppermute | solution.py:293
  913.2 183.6 %collective-permute-start.13 = (bf16[1024,2048]{1,0:T(8,128)(2,1)}, bf16[1024,2048]{1,0:T(8,128)(2,1)}, u32[]{:S(2)}, u32[]{:S(2)}) collective-permute-start(bf16[1024,2048]{1,0:T(8,128)(2,1)} %get-tuple-element.86.refs_6_.refs_7_), channel_id=1, source_target_pairs={{0,2},{2,0},{1,3},{3,1},{4,6},{6,4},{5,7},{7,5}} | collective-permute-start | bytes 12582920 | tf_op jit(solution)/shard_map/ppermute | solution.py:293
  915.2 181.6 %collective-permute-start.14 = (bf16[1024,4096]{1,0:T(8,128)(2,1)}, bf16[1024,4096]{1,0:T(8,128)(2,1)}, u32[]{:S(2)}, u32[]{:S(2)}) collective-permute-start(bf16[1024,4096]{1,0:T(8,128)(2,1)} %collective-permute-done.8.refs_0_.refs_1_), channel_id=1, source_target_pairs={{0,1},{1,0},{2,3},{3,2},{4,5},{5,4},{6,7},{7,6}} | collective-permute-start | bytes 25165832 | tf_op jit(solution)/shard_map/ppermute | solution.py:290
  967.0 24.8 %collective-permute-start.17 = (bf16[1024,256]{1,0:T(8,128)(2,1)S(1)}, bf16[1024,256]{1,0:T(8,128)(2,1)S(1)}, u32[]{:S(2)}, u32[]{:S(2)}) collective-permute-start(bf16[1024,256]{1,0:T(8,128)(2,1)S(1)} %get-tuple-element.148.refs_6_.refs_7_), channel_id=1, source_target_pairs={{0,1},{1,0},{2,3},{3,2},{4,5},{5,4},{6,7},{7,6}} | collective-permute-start | bytes 1572872 | tf_op jit(solution)/shard_map/ppermute | solution.py:290
  991.7 136.9 %collective-permute-start.21 = (bf16[2048,256]{1,0:T(8,128)(2,1)}, bf16[2048,256]{1,0:T(8,128)(2,1)}, u32[]{:S(2)}, u32[]{:S(2)}) collective-permute-start(bf16[2048,256]{1,0:T(8,128)(2,1)} %pad_maximum_fusion.3), channel_id=1, source_target_pairs={{0,2},{2,0},{1,3},{3,1},{4,6},{6,4},{5,7},{7,5}} | collective-permute-start | bytes 3145736 | tf_op jit(solution)/shard_map/ppermute | solution.py:293
  1128.6 74.5 %collective-permute-start.23 = (f32[4096,1024]{1,0:T(8,128)}, f32[4096,1024]{1,0:T(8,128)}, u32[]{:S(2)}, u32[]{:S(2)}) collective-permute-start(f32[4096,1024]{1,0:T(8,128)} %get-tuple-element.106), channel_id=1, source_target_pairs={{0,1},{1,0},{2,3},{3,2},{4,5},{5,4},{6,7},{7,6}} | collective-permute-start | bytes 50331656 | tf_op jit(solution)/shard_map/ppermute | solution.py:290
  1160.6 57.0 %collective-permute-start.22 = (f32[4096,1024]{1,0:T(8,128)}, f32[4096,1024]{1,0:T(8,128)}, u32[]{:S(2)}, u32[]{:S(2)}) collective-permute-start(f32[4096,1024]{1,0:T(8,128)} %get-tuple-element.105), channel_id=1, source_target_pairs={{0,1},{1,0},{2,3},{3,2},{4,5},{5,4},{6,7},{7,6}} | collective-permute-start | bytes 50331656 | tf_op jit(solution)/shard_map/ppermute | solution.py:290
  1176.2 20.4 %collective-permute-start.24 = (f32[4096,256]{1,0:T(8,128)}, f32[4096,256]{1,0:T(8,128)}, u32[]{:S(2)}, u32[]{:S(2)}) collective-permute-start(f32[4096,256]{1,0:T(8,128)} %shard_map.127), channel_id=1, source_target_pairs={{0,1},{1,0},{2,3},{3,2},{4,5},{5,4},{6,7},{7,6}} | collective-permute-start | bytes 12582920 | tf_op jit(solution)/shard_map/ppermute | solution.py:290
  1176.3 15.9 %collective-permute-start.19 = (f32[4096]{0:T(1024)S(1)}, f32[4096]{0:T(1024)S(1)}, u32[]{:S(2)}, u32[]{:S(2)}) collective-permute-start(f32[4096]{0:T(1024)S(1)} %get-tuple-element.112), channel_id=1, source_target_pairs={{0,1},{1,0},{2,3},{3,2},{4,5},{5,4},{6,7},{7,6}} | collective-permute-start | bytes 49160 | tf_op jit(solution)/shard_map/ppermute | solution.py:290
  (32 other events, 544.3 us)
